TPU v7x, 256 devices: a whole 4x4x8 slice. The times are simulated.
256 devices in a mesh: rep: 4 (over z_hi, core), dom: 64 (over z_lo, y, x).
Axes of the slice: x: 4, y: 4, z: 8 (z_hi: 2, z_lo: 4; z = z_hi * 4 + z_lo), core: 2. Of those that a mesh axis runs over, the one named last changes fastest.
Arguments:
- positions: float32 [3, 2097152], P(None, ('rep', 'dom')), parts along dimension 1, may hold values from -4 to 4
- velocities: float32 [3, 2097152], P(None, ('rep', 'dom')), parts along dimension 1, may hold values from -5 to 5
- charges: float32 [2097152], P(('rep', 'dom')), parts along dimension 0, may hold values from -4 to 4
- solute: int32 [2097152], P(('rep', 'dom')), parts along dimension 0, may hold values 0 or 1
- rest_scale: float32 [4], P('rep'), parts along dimension 0, may hold values from 0.25 to 1
- send_slot: int32 [256, 64], P(('rep', 'dom')), parts along dimension 0, may hold values from 0 to 64, as said below
- land_slot: int32 [256, 64], P(('rep', 'dom')), parts along dimension 0, may hold values from 0 to 64, as said below
- ghost_slot: int32 [256, 64], P(('rep', 'dom')), parts along dimension 0, may hold values from 0 to 63
- pair_home: int32 [256, 192], P(('rep', 'dom')), parts along dimension 0, may hold values from 0 to 63
- pair_other: int32 [256, 192], P(('rep', 'dom')), parts along dimension 0, may hold values from 0 to 127, as said below
Outputs:
- positions_out: float32 [3, 2097152], P(None, ('rep', 'dom')), parts along dimension 1
- velocities_out: float32 [3, 2097152], P(None, ('rep', 'dom')), parts along dimension 1
- forces_out: float32 [3, 2097152], P(None, ('rep', 'dom')), parts along dimension 1
There are 4 independent parts, one for each index of `rep`. A program takes and returns all parts, laid end to end along the dimension named above; each array names one. Nothing has to cross between parts.
Inputs may be any that keep to these rules, and one draw needn't show every extreme that they name: `send_slot`: entry [d, p] is the slot of the block domain d hands to domain p, or 64 where it hands none; each domain hands 32 distinct blocks to 32 distinct other domains, and each domain receives from 32 domains. `land_slot`: entry [d, p] is the slot that the block arriving at d from p takes, or 64 exactly where send_slot[p, d] is 64; the slots a domain fills are exactly the slots it hands over. `pair_other`: in every row the first 128 entries are below 64; the other 64 are 64 or more, and every ghost slot appears among them at least once.
All inputs are finite; a program needn't handle non-finite values. No bound on the sum of `solute` on one device may be relied on, other than what follows from the above.
Results may differ from a plain program's by a relative error of at most 0.0001.
Values sent between devices are 32-bit elements; how exact they have to be, the bound alone decides.
No kernel may reach another device: no remote copies, remote signals or barrier semaphores. Data moves between devices by JAX's collectives and lax.ppermute only.
A program may use at most 64 MiB of HBM per device.

v0:
```python
import jax
import jax.numpy as jnp
from jax import lax
from jax.sharding import PartitionSpec as P

BLOCK = 128
STEPS = 2


coupling_scale = 0.2
time_step = 0.05
highest = lax.Precision.HIGHEST
tile_group = 16


def tile_forces(left_coords, left_params, right_coords, right_params):
    inner = lax.dot_general(
        left_coords,
        right_coords,
        (((0,), (0,)), ((), ())),
        precision=highest,
        preferred_element_type=jnp.float32,
    )
    squared = (
        jnp.sum(left_coords * left_coords, 0)[:, None]
        + jnp.sum(right_coords * right_coords, 0)[None, :]
        - 2.0 * inner
    )
    decay = jnp.exp(-0.5 * squared)
    coupling = coupling_scale * (
        left_params[0][:, None] * right_params[0][None, :] * decay
        + left_params[1][:, None] * right_params[1][None, :] * decay * decay
    )
    left_force = left_coords * jnp.sum(coupling, 1)[None, :] - lax.dot_general(
        right_coords,
        coupling,
        (((1,), (1,)), ((), ())),
        precision=highest,
        preferred_element_type=jnp.float32,
    )
    right_force = right_coords * jnp.sum(coupling, 0)[None, :] - jnp.dot(
        left_coords, coupling, precision=highest, preferred_element_type=jnp.float32
    )
    return (left_force, right_force)


def pair_forces(home_coords, home_params, other_coords, other_params):
    tile_count = home_coords.shape[0]

    def one_group(operands):
        return jax.vmap(tile_forces)(*operands)

    shaped = tuple(
        (
            operand.reshape((tile_count // tile_group, tile_group) + operand.shape[1:])
            for operand in (home_coords, home_params, other_coords, other_params)
        )
    )
    home_force, other_force = lax.map(one_group, shaped)
    return (home_force.reshape(home_coords.shape), other_force.reshape(other_coords.shape))


def accumulate(indices, values, row_count):
    onehot = (
        lax.broadcasted_iota(jnp.int32, (row_count, indices.shape[0]), 0) == indices[None, :]
    ).astype(jnp.float32)
    flattened = values.reshape(values.shape[0], -1)
    summed = jnp.dot(onehot, flattened, precision=highest, preferred_element_type=jnp.float32)
    return summed.reshape((row_count,) + values.shape[1:])


def on_device(
    positions,
    velocities,
    charges,
    solute,
    rest_scale,
    send_slot,
    land_slot,
    ghost_slot,
    pair_home,
    pair_other,
):
    blocks = positions.shape[1] // BLOCK
    weight = jnp.where(solute == 1, jnp.sqrt(rest_scale[0]), 1.0)
    params = jnp.stack([weight * charges, weight])
    states = (
        jnp.concatenate([positions, velocities, params], 0)
        .reshape(8, blocks, BLOCK)
        .transpose(1, 0, 2)
    )
    padded = jnp.concatenate([states, jnp.zeros((1, 8, BLOCK), jnp.float32)], 0)
    outbound = jnp.take(padded, send_slot[0], axis=0)
    arrived = lax.all_to_all(outbound, "dom", split_axis=0, concat_axis=0, tiled=True)
    placed = padded.at[land_slot[0]].set(arrived)[:blocks]
    coords = placed[:, :3]
    speeds = placed[:, 3:6]
    params_now = placed[:, 6:]
    home_rows = pair_home[0]
    other_rows = pair_other[0]
    send_rows = ghost_slot[0]
    ghost_params = params_now
    forces = jnp.zeros_like(coords)
    for step_index in range(STEPS):
        if step_index == 0:
            outgoing = jnp.take(jnp.concatenate([coords, params_now], 1), send_rows, axis=0)
            ghosts = lax.all_to_all(outgoing, "dom", split_axis=0, concat_axis=0, tiled=True)
            ghost_coords = ghosts[:, :3]
            ghost_params = ghosts[:, 3:]
        else:
            ghost_coords = lax.all_to_all(
                jnp.take(coords, send_rows, axis=0), "dom", split_axis=0, concat_axis=0, tiled=True
            )
        ghost_count = ghost_coords.shape[0]
        table_coords = jnp.concatenate([coords, ghost_coords], 0)
        table_params = jnp.concatenate([params_now, ghost_params], 0)
        home_force, other_force = pair_forces(
            jnp.take(table_coords, home_rows, axis=0),
            jnp.take(table_params, home_rows, axis=0),
            jnp.take(table_coords, other_rows, axis=0),
            jnp.take(table_params, other_rows, axis=0),
        )
        summed = accumulate(home_rows, home_force, blocks + ghost_count) + accumulate(
            other_rows, other_force, blocks + ghost_count
        )
        forces = summed[:blocks]
        ghost_forces = summed[blocks:]
        returned = lax.all_to_all(ghost_forces, "dom", split_axis=0, concat_axis=0, tiled=True)
        forces = forces + accumulate(send_rows, returned, blocks)
        speeds = speeds + time_step * forces
        coords = coords + time_step * speeds

    def flatten(values):
        return values.transpose(1, 0, 2).reshape(3, blocks * BLOCK)

    return (flatten(coords), flatten(speeds), flatten(forces))


def solution(mesh):
    in_specs = (
        P(None, ("rep", "dom")),
        P(None, ("rep", "dom")),
        P(("rep", "dom")),
        P(("rep", "dom")),
        P("rep"),
        P(("rep", "dom"), None),
        P(("rep", "dom"), None),
        P(("rep", "dom"), None),
        P(("rep", "dom"), None),
        P(("rep", "dom"), None),
    )
    out_specs = (P(None, ("rep", "dom")), P(None, ("rep", "dom")), P(None, ("rep", "dom")))
    return jax.shard_map(
        on_device, mesh=mesh, in_specs=in_specs, out_specs=out_specs, check_vma=False
    )
```

profile of v0, /device:TPU:2, one launch (start us, length us, event | category | flops | bytes accessed | tf_op | source)
XLA Modules:
  0.0 255.7 jit_solution(11290231723534257404)
XLA Ops:
  2.9 1.0 maximum_bitcast_fusion
  5.4 12.2 %all-to-all-start = ((f32[64,8,128]{2,1,0:T(8,128)}), f32[64,8,128]{2,1,0:T(8,128)S(1)}, u32[]{:S(2)}, u32[]{:S(2)}) async-start(f32[64,8,128]{2,1,0:T(8,128)} %broadcast_select_fusion.7), calls=%async_computation | async-start | bytes 524288 | tf_op jit(solution)/shard_map/all_to_all | solution.py:94
  19.7 9.5 %all-to-all-done = f32[64,8,128]{2,1,0:T(8,128)S(1)} async-done(((f32[64,8,128]{2,1,0:T(8,128)}), f32[64,8,128]{2,1,0:T(8,128)S(1)}, u32[]{:S(2)}, u32[]{:S(2)}) %all-to-all-start) | async-done | bytes 262176 | tf_op jit(solution)/shard_map/all_to_all | solution.py:94
  29.2 2.5 scatter_fusion
  33.4 6.0 %all-to-all-start.1 = ((f32[64,5,128]{2,1,0:T(8,128)}), f32[64,5,128]{2,1,0:T(8,128)S(1)}, u32[]{:S(2)}, u32[]{:S(2)}) async-start(f32[64,5,128]{2,1,0:T(8,128)} %broadcast_select_fusion.6), calls=%async_computation.1 | async-start | bytes 524288 | tf_op jit(solution)/shard_map/all_to_all | solution.py:107
  39.5 11.1 %all-to-all-done.1 = f32[64,5,128]{2,1,0:T(8,128)S(1)} async-done(((f32[64,5,128]{2,1,0:T(8,128)}), f32[64,5,128]{2,1,0:T(8,128)S(1)}, u32[]{:S(2)}, u32[]{:S(2)}) %all-to-all-start.1) | async-done | bytes 163872 | tf_op jit(solution)/shard_map/all_to_all | solution.py:107
  55.8 73.7 %while.24 = (s32[]{:T(128)}, f32[12,16,3,128]{3,2,1,0:T(4,128)S(1)}, f32[12,16,3,128]{3,2,1,0:T(4,128)S(1)}, f32[12,16,3,128]{3,2,1,0:T(4,128)S(1)}, f32[12,16,2...) while((s32[]{:T(128)}, ...), condition=%wide.region_6.9_spmd, body=%wide.region_1.8_spmd.sunk | while | flops 31498240 | bytes 3689565 | solution.py:59
  55.9 3.3 %fusion.104 = (f32[16,128]{1,0:T(8,128)S(1)}, f32[16,128]{1,0:T(8,128)S(1)}, f32[16,128,128]{2,1,0:T(8,128)S(1)}) fusion(f32[12,16,3,128]{3,2,1,0:T(4,128)S(1)} %get-tuple-element.339, s32[]{:T(128)} %get-tuple-element.325, f32[12,16,3,128]{3,2,1,0:T(4,128)S(1)} %get-tuple-element.336, f32[16,128]{1,0:T(8,128)S(1)} %get-tuple-element.288, ...), kind=kOutput, calls=%fused_computation.156.clone.1 | convolution fusion | flops 12578816 | bytes 1180672 | tf_op jit(solution)/shard_map/while/body/eval_jaxpr/vmap()/dot_general | solution.py:17
  59.2 1.0 fusion.106
  60.1 1.8 fusion.105
  62.0 3.3 %fusion.104 = (f32[16,128]{1,0:T(8,128)S(1)}, f32[16,128]{1,0:T(8,128)S(1)}, f32[16,128,128]{2,1,0:T(8,128)S(1)}) fusion(f32[12,16,3,128]{3,2,1,0:T(4,128)S(1)} %get-tuple-element.339, s32[]{:T(128)} %get-tuple-element.325, f32[12,16,3,128]{3,2,1,0:T(4,128)S(1)} %get-tuple-element.336, f32[16,128]{1,0:T(8,128)S(1)} %get-tuple-element.288, ...), kind=kOutput, calls=%fused_computation.156.clone.1 | convolution fusion | flops 12578816 | bytes 1180672 | tf_op jit(solution)/shard_map/while/body/eval_jaxpr/vmap()/dot_general | solution.py:17
  66.3 1.8 fusion.105
  68.2 3.3 %fusion.104 = (f32[16,128]{1,0:T(8,128)S(1)}, f32[16,128]{1,0:T(8,128)S(1)}, f32[16,128,128]{2,1,0:T(8,128)S(1)}) fusion(f32[12,16,3,128]{3,2,1,0:T(4,128)S(1)} %get-tuple-element.339, s32[]{:T(128)} %get-tuple-element.325, f32[12,16,3,128]{3,2,1,0:T(4,128)S(1)} %get-tuple-element.336, f32[16,128]{1,0:T(8,128)S(1)} %get-tuple-element.288, ...), kind=kOutput, calls=%fused_computation.156.clone.1 | convolution fusion | flops 12578816 | bytes 1180672 | tf_op jit(solution)/shard_map/while/body/eval_jaxpr/vmap()/dot_general | solution.py:17
  71.4 1.0 fusion.106
  72.4 1.8 fusion.105
  74.3 3.3 %fusion.104 = (f32[16,128]{1,0:T(8,128)S(1)}, f32[16,128]{1,0:T(8,128)S(1)}, f32[16,128,128]{2,1,0:T(8,128)S(1)}) fusion(f32[12,16,3,128]{3,2,1,0:T(4,128)S(1)} %get-tuple-element.339, s32[]{:T(128)} %get-tuple-element.325, f32[12,16,3,128]{3,2,1,0:T(4,128)S(1)} %get-tuple-element.336, f32[16,128]{1,0:T(8,128)S(1)} %get-tuple-element.288, ...), kind=kOutput, calls=%fused_computation.156.clone.1 | convolution fusion | flops 12578816 | bytes 1180672 | tf_op jit(solution)/shard_map/while/body/eval_jaxpr/vmap()/dot_general | solution.py:17
  77.6 1.0 fusion.106
  78.6 1.8 fusion.105
  80.4 3.3 %fusion.104 = (f32[16,128]{1,0:T(8,128)S(1)}, f32[16,128]{1,0:T(8,128)S(1)}, f32[16,128,128]{2,1,0:T(8,128)S(1)}) fusion(f32[12,16,3,128]{3,2,1,0:T(4,128)S(1)} %get-tuple-element.339, s32[]{:T(128)} %get-tuple-element.325, f32[12,16,3,128]{3,2,1,0:T(4,128)S(1)} %get-tuple-element.336, f32[16,128]{1,0:T(8,128)S(1)} %get-tuple-element.288, ...), kind=kOutput, calls=%fused_computation.156.clone.1 | convolution fusion | flops 12578816 | bytes 1180672 | tf_op jit(solution)/shard_map/while/body/eval_jaxpr/vmap()/dot_general | solution.py:17
  83.7 1.0 fusion.106
  84.7 1.8 fusion.105
  86.6 3.3 %fusion.104 = (f32[16,128]{1,0:T(8,128)S(1)}, f32[16,128]{1,0:T(8,128)S(1)}, f32[16,128,128]{2,1,0:T(8,128)S(1)}) fusion(f32[12,16,3,128]{3,2,1,0:T(4,128)S(1)} %get-tuple-element.339, s32[]{:T(128)} %get-tuple-element.325, f32[12,16,3,128]{3,2,1,0:T(4,128)S(1)} %get-tuple-element.336, f32[16,128]{1,0:T(8,128)S(1)} %get-tuple-element.288, ...), kind=kOutput, calls=%fused_computation.156.clone.1 | convolution fusion | flops 12578816 | bytes 1180672 | tf_op jit(solution)/shard_map/while/body/eval_jaxpr/vmap()/dot_general | solution.py:17
  89.9 1.0 fusion.106
  90.9 1.8 fusion.105
  92.7 3.3 %fusion.104 = (f32[16,128]{1,0:T(8,128)S(1)}, f32[16,128]{1,0:T(8,128)S(1)}, f32[16,128,128]{2,1,0:T(8,128)S(1)}) fusion(f32[12,16,3,128]{3,2,1,0:T(4,128)S(1)} %get-tuple-element.339, s32[]{:T(128)} %get-tuple-element.325, f32[12,16,3,128]{3,2,1,0:T(4,128)S(1)} %get-tuple-element.336, f32[16,128]{1,0:T(8,128)S(1)} %get-tuple-element.288, ...), kind=kOutput, calls=%fused_computation.156.clone.1 | convolution fusion | flops 12578816 | bytes 1180672 | tf_op jit(solution)/shard_map/while/body/eval_jaxpr/vmap()/dot_general | solution.py:17
  97.0 1.8 fusion.105
  98.9 3.3 %fusion.104 = (f32[16,128]{1,0:T(8,128)S(1)}, f32[16,128]{1,0:T(8,128)S(1)}, f32[16,128,128]{2,1,0:T(8,128)S(1)}) fusion(f32[12,16,3,128]{3,2,1,0:T(4,128)S(1)} %get-tuple-element.339, s32[]{:T(128)} %get-tuple-element.325, f32[12,16,3,128]{3,2,1,0:T(4,128)S(1)} %get-tuple-element.336, f32[16,128]{1,0:T(8,128)S(1)} %get-tuple-element.288, ...), kind=kOutput, calls=%fused_computation.156.clone.1 | convolution fusion | flops 12578816 | bytes 1180672 | tf_op jit(solution)/shard_map/while/body/eval_jaxpr/vmap()/dot_general | solution.py:17
  103.2 1.8 fusion.105
  105.0 3.3 %fusion.104 = (f32[16,128]{1,0:T(8,128)S(1)}, f32[16,128]{1,0:T(8,128)S(1)}, f32[16,128,128]{2,1,0:T(8,128)S(1)}) fusion(f32[12,16,3,128]{3,2,1,0:T(4,128)S(1)} %get-tuple-element.339, s32[]{:T(128)} %get-tuple-element.325, f32[12,16,3,128]{3,2,1,0:T(4,128)S(1)} %get-tuple-element.336, f32[16,128]{1,0:T(8,128)S(1)} %get-tuple-element.288, ...), kind=kOutput, calls=%fused_computation.156.clone.1 | convolution fusion | flops 12578816 | bytes 1180672 | tf_op jit(solution)/shard_map/while/body/eval_jaxpr/vmap()/dot_general | solution.py:17
  109.3 1.8 fusion.105
  111.2 3.3 %fusion.104 = (f32[16,128]{1,0:T(8,128)S(1)}, f32[16,128]{1,0:T(8,128)S(1)}, f32[16,128,128]{2,1,0:T(8,128)S(1)}) fusion(f32[12,16,3,128]{3,2,1,0:T(4,128)S(1)} %get-tuple-element.339, s32[]{:T(128)} %get-tuple-element.325, f32[12,16,3,128]{3,2,1,0:T(4,128)S(1)} %get-tuple-element.336, f32[16,128]{1,0:T(8,128)S(1)} %get-tuple-element.288, ...), kind=kOutput, calls=%fused_computation.156.clone.1 | convolution fusion | flops 12578816 | bytes 1180672 | tf_op jit(solution)/shard_map/while/body/eval_jaxpr/vmap()/dot_general | solution.py:17
  115.4 1.8 fusion.105
  117.3 3.3 %fusion.104 = (f32[16,128]{1,0:T(8,128)S(1)}, f32[16,128]{1,0:T(8,128)S(1)}, f32[16,128,128]{2,1,0:T(8,128)S(1)}) fusion(f32[12,16,3,128]{3,2,1,0:T(4,128)S(1)} %get-tuple-element.339, s32[]{:T(128)} %get-tuple-element.325, f32[12,16,3,128]{3,2,1,0:T(4,128)S(1)} %get-tuple-element.336, f32[16,128]{1,0:T(8,128)S(1)} %get-tuple-element.288, ...), kind=kOutput, calls=%fused_computation.156.clone.1 | convolution fusion | flops 12578816 | bytes 1180672 | tf_op jit(solution)/shard_map/while/body/eval_jaxpr/vmap()/dot_general | solution.py:17
  121.6 1.8 fusion.105
  123.5 3.3 %fusion.104 = (f32[16,128]{1,0:T(8,128)S(1)}, f32[16,128]{1,0:T(8,128)S(1)}, f32[16,128,128]{2,1,0:T(8,128)S(1)}) fusion(f32[12,16,3,128]{3,2,1,0:T(4,128)S(1)} %get-tuple-element.339, s32[]{:T(128)} %get-tuple-element.325, f32[12,16,3,128]{3,2,1,0:T(4,128)S(1)} %get-tuple-element.336, f32[16,128]{1,0:T(8,128)S(1)} %get-tuple-element.288, ...), kind=kOutput, calls=%fused_computation.156.clone.1 | convolution fusion | flops 12578816 | bytes 1180672 | tf_op jit(solution)/shard_map/while/body/eval_jaxpr/vmap()/dot_general | solution.py:17
  127.7 1.8 fusion.105
  130.4 15.6 %all_to_all.25 = f32[64,3,128]{2,1,0:T(4,128)S(1)} all-to-all(f32[64,3,128]{2,1,0:T(4,128)S(1)} %copy.60), channel_id=1, replica_groups=mesh['rep'=4,'dom'=64] {'dom'}, dimensions={0} | all-to-all | bytes 196608 | tf_op jit(solution)/shard_map/all_to_all | solution.py:128
  147.1 14.8 %all_to_all.26 = f32[64,3,128]{2,1,0:T(4,128)S(1)} all-to-all(f32[64,3,128]{2,1,0:T(4,128)S(1)} %broadcast_select_fusion.8), channel_id=1, replica_groups=mesh['rep'=4,'dom'=64] {'dom'}, dimensions={0} | all-to-all | bytes 196608 | tf_op jit(solution)/shard_map/all_to_all | solution.py:111
  164.5 73.7 %while.25 = (s32[]{:T(128)}, f32[12,16,3,128]{3,2,1,0:T(4,128)S(1)}, f32[12,16,3,128]{3,2,1,0:T(4,128)S(1)}, f32[12,16,3,128]{3,2,1,0:T(4,128)S(1)}, f32[12,16,2...) while((s32[]{:T(128)}, ...), condition=%wide.region_12.15_spmd, body=%wide.region_7.14_spmd.sunk | while | flops 31498240 | bytes 3689565 | solution.py:59
  164.7 3.3 %fusion.112 = (f32[16,128]{1,0:T(8,128)S(1)}, f32[16,128]{1,0:T(8,128)S(1)}, f32[16,128,128]{2,1,0:T(8,128)S(1)}) fusion(f32[12,16,3,128]{3,2,1,0:T(4,128)S(1)} %get-tuple-element.363, s32[]{:T(128)} %get-tuple-element.349, f32[12,16,3,128]{3,2,1,0:T(4,128)S(1)} %get-tuple-element.360, f32[16,128]{1,0:T(8,128)S(1)} %get-tuple-element.306, ...), kind=kOutput, calls=%fused_computation.157.clone.1 | convolution fusion | flops 12578816 | bytes 1180672 | tf_op jit(solution)/shard_map/while/body/eval_jaxpr/vmap()/dot_general | solution.py:17
  168.9 1.8 fusion.113
  170.8 3.3 %fusion.112 = (f32[16,128]{1,0:T(8,128)S(1)}, f32[16,128]{1,0:T(8,128)S(1)}, f32[16,128,128]{2,1,0:T(8,128)S(1)}) fusion(f32[12,16,3,128]{3,2,1,0:T(4,128)S(1)} %get-tuple-element.363, s32[]{:T(128)} %get-tuple-element.349, f32[12,16,3,128]{3,2,1,0:T(4,128)S(1)} %get-tuple-element.360, f32[16,128]{1,0:T(8,128)S(1)} %get-tuple-element.306, ...), kind=kOutput, calls=%fused_computation.157.clone.1 | convolution fusion | flops 12578816 | bytes 1180672 | tf_op jit(solution)/shard_map/while/body/eval_jaxpr/vmap()/dot_general | solution.py:17
  175.1 1.8 fusion.113
  176.9 3.3 %fusion.112 = (f32[16,128]{1,0:T(8,128)S(1)}, f32[16,128]{1,0:T(8,128)S(1)}, f32[16,128,128]{2,1,0:T(8,128)S(1)}) fusion(f32[12,16,3,128]{3,2,1,0:T(4,128)S(1)} %get-tuple-element.363, s32[]{:T(128)} %get-tuple-element.349, f32[12,16,3,128]{3,2,1,0:T(4,128)S(1)} %get-tuple-element.360, f32[16,128]{1,0:T(8,128)S(1)} %get-tuple-element.306, ...), kind=kOutput, calls=%fused_computation.157.clone.1 | convolution fusion | flops 12578816 | bytes 1180672 | tf_op jit(solution)/shard_map/while/body/eval_jaxpr/vmap()/dot_general | solution.py:17
  181.2 1.8 fusion.113
  183.1 3.3 %fusion.112 = (f32[16,128]{1,0:T(8,128)S(1)}, f32[16,128]{1,0:T(8,128)S(1)}, f32[16,128,128]{2,1,0:T(8,128)S(1)}) fusion(f32[12,16,3,128]{3,2,1,0:T(4,128)S(1)} %get-tuple-element.363, s32[]{:T(128)} %get-tuple-element.349, f32[12,16,3,128]{3,2,1,0:T(4,128)S(1)} %get-tuple-element.360, f32[16,128]{1,0:T(8,128)S(1)} %get-tuple-element.306, ...), kind=kOutput, calls=%fused_computation.157.clone.1 | convolution fusion | flops 12578816 | bytes 1180672 | tf_op jit(solution)/shard_map/while/body/eval_jaxpr/vmap()/dot_general | solution.py:17
  187.4 1.8 fusion.113
  189.2 3.3 %fusion.112 = (f32[16,128]{1,0:T(8,128)S(1)}, f32[16,128]{1,0:T(8,128)S(1)}, f32[16,128,128]{2,1,0:T(8,128)S(1)}) fusion(f32[12,16,3,128]{3,2,1,0:T(4,128)S(1)} %get-tuple-element.363, s32[]{:T(128)} %get-tuple-element.349, f32[12,16,3,128]{3,2,1,0:T(4,128)S(1)} %get-tuple-element.360, f32[16,128]{1,0:T(8,128)S(1)} %get-tuple-element.306, ...), kind=kOutput, calls=%fused_computation.157.clone.1 | convolution fusion | flops 12578816 | bytes 1180672 | tf_op jit(solution)/shard_map/while/body/eval_jaxpr/vmap()/dot_general | solution.py:17
  193.5 1.8 fusion.113
  195.4 3.3 %fusion.112 = (f32[16,128]{1,0:T(8,128)S(1)}, f32[16,128]{1,0:T(8,128)S(1)}, f32[16,128,128]{2,1,0:T(8,128)S(1)}) fusion(f32[12,16,3,128]{3,2,1,0:T(4,128)S(1)} %get-tuple-element.363, s32[]{:T(128)} %get-tuple-element.349, f32[12,16,3,128]{3,2,1,0:T(4,128)S(1)} %get-tuple-element.360, f32[16,128]{1,0:T(8,128)S(1)} %get-tuple-element.306, ...), kind=kOutput, calls=%fused_computation.157.clone.1 | convolution fusion | flops 12578816 | bytes 1180672 | tf_op jit(solution)/shard_map/while/body/eval_jaxpr/vmap()/dot_general | solution.py:17
  199.7 1.8 fusion.113
  201.5 3.3 %fusion.112 = (f32[16,128]{1,0:T(8,128)S(1)}, f32[16,128]{1,0:T(8,128)S(1)}, f32[16,128,128]{2,1,0:T(8,128)S(1)}) fusion(f32[12,16,3,128]{3,2,1,0:T(4,128)S(1)} %get-tuple-element.363, s32[]{:T(128)} %get-tuple-element.349, f32[12,16,3,128]{3,2,1,0:T(4,128)S(1)} %get-tuple-element.360, f32[16,128]{1,0:T(8,128)S(1)} %get-tuple-element.306, ...), kind=kOutput, calls=%fused_computation.157.clone.1 | convolution fusion | flops 12578816 | bytes 1180672 | tf_op jit(solution)/shard_map/while/body/eval_jaxpr/vmap()/dot_general | solution.py:17
  205.8 1.8 fusion.113
  207.7 3.3 %fusion.112 = (f32[16,128]{1,0:T(8,128)S(1)}, f32[16,128]{1,0:T(8,128)S(1)}, f32[16,128,128]{2,1,0:T(8,128)S(1)}) fusion(f32[12,16,3,128]{3,2,1,0:T(4,128)S(1)} %get-tuple-element.363, s32[]{:T(128)} %get-tuple-element.349, f32[12,16,3,128]{3,2,1,0:T(4,128)S(1)} %get-tuple-element.360, f32[16,128]{1,0:T(8,128)S(1)} %get-tuple-element.306, ...), kind=kOutput, calls=%fused_computation.157.clone.1 | convolution fusion | flops 12578816 | bytes 1180672 | tf_op jit(solution)/shard_map/while/body/eval_jaxpr/vmap()/dot_general | solution.py:17
  212.0 1.8 fusion.113
  213.8 3.3 %fusion.112 = (f32[16,128]{1,0:T(8,128)S(1)}, f32[16,128]{1,0:T(8,128)S(1)}, f32[16,128,128]{2,1,0:T(8,128)S(1)}) fusion(f32[12,16,3,128]{3,2,1,0:T(4,128)S(1)} %get-tuple-element.363, s32[]{:T(128)} %get-tuple-element.349, f32[12,16,3,128]{3,2,1,0:T(4,128)S(1)} %get-tuple-element.360, f32[16,128]{1,0:T(8,128)S(1)} %get-tuple-element.306, ...), kind=kOutput, calls=%fused_computation.157.clone.1 | convolution fusion | flops 12578816 | bytes 1180672 | tf_op jit(solution)/shard_map/while/body/eval_jaxpr/vmap()/dot_general | solution.py:17
  218.1 1.8 fusion.113
  220.0 3.3 %fusion.112 = (f32[16,128]{1,0:T(8,128)S(1)}, f32[16,128]{1,0:T(8,128)S(1)}, f32[16,128,128]{2,1,0:T(8,128)S(1)}) fusion(f32[12,16,3,128]{3,2,1,0:T(4,128)S(1)} %get-tuple-element.363, s32[]{:T(128)} %get-tuple-element.349, f32[12,16,3,128]{3,2,1,0:T(4,128)S(1)} %get-tuple-element.360, f32[16,128]{1,0:T(8,128)S(1)} %get-tuple-element.306, ...), kind=kOutput, calls=%fused_computation.157.clone.1 | convolution fusion | flops 12578816 | bytes 1180672 | tf_op jit(solution)/shard_map/while/body/eval_jaxpr/vmap()/dot_general | solution.py:17
  224.2 1.8 fusion.113
  226.1 3.3 %fusion.112 = (f32[16,128]{1,0:T(8,128)S(1)}, f32[16,128]{1,0:T(8,128)S(1)}, f32[16,128,128]{2,1,0:T(8,128)S(1)}) fusion(f32[12,16,3,128]{3,2,1,0:T(4,128)S(1)} %get-tuple-element.363, s32[]{:T(128)} %get-tuple-element.349, f32[12,16,3,128]{3,2,1,0:T(4,128)S(1)} %get-tuple-element.360, f32[16,128]{1,0:T(8,128)S(1)} %get-tuple-element.306, ...), kind=kOutput, calls=%fused_computation.157.clone.1 | convolution fusion | flops 12578816 | bytes 1180672 | tf_op jit(solution)/shard_map/while/body/eval_jaxpr/vmap()/dot_general | solution.py:17
  230.4 1.8 fusion.113
  232.2 3.3 %fusion.112 = (f32[16,128]{1,0:T(8,128)S(1)}, f32[16,128]{1,0:T(8,128)S(1)}, f32[16,128,128]{2,1,0:T(8,128)S(1)}) fusion(f32[12,16,3,128]{3,2,1,0:T(4,128)S(1)} %get-tuple-element.363, s32[]{:T(128)} %get-tuple-element.349, f32[12,16,3,128]{3,2,1,0:T(4,128)S(1)} %get-tuple-element.360, f32[16,128]{1,0:T(8,128)S(1)} %get-tuple-element.306, ...), kind=kOutput, calls=%fused_computation.157.clone.1 | convolution fusion | flops 12578816 | bytes 1180672 | tf_op jit(solution)/shard_map/while/body/eval_jaxpr/vmap()/dot_general | solution.py:17
  236.5 1.8 fusion.113
  239.2 14.7 %all_to_all.27 = f32[64,3,128]{2,1,0:T(4,128)S(1)} all-to-all(f32[64,3,128]{2,1,0:T(4,128)S(1)} %copy.70), channel_id=1, replica_groups=mesh['rep'=4,'dom'=64] {'dom'}, dimensions={0} | all-to-all | bytes 196608 | tf_op jit(solution)/shard_map/all_to_all | solution.py:128
  (197 shorter events, 39.3 us)
Async XLA Ops:
  0.6 0.7 copy-start.4
  0.6 2.2 copy-start
  5.4 12.2 %copy-start.3 = (s32[1,64]{1,0:T(1,128)S(1)}, s32[1,64]{1,0:T(1,128)}, u32[]{:S(2)}) copy-start(s32[1,64]{1,0:T(1,128)} %param.25) | copy-start | bytes 772
  5.4 23.8 %all-to-all-start = ((f32[64,8,128]{2,1,0:T(8,128)}), f32[64,8,128]{2,1,0:T(8,128)S(1)}, u32[]{:S(2)}, u32[]{:S(2)}) async-start(f32[64,8,128]{2,1,0:T(8,128)} %broadcast_select_fusion.7), calls=%async_computation | async-start | bytes 524288 | tf_op jit(solution)/shard_map/all_to_all | solution.py:94
  17.6 0.7 copy-start.5
  18.3 0.7 copy-start.1
  19.0 0.7 copy-start.2
  33.4 17.2 %all-to-all-start.1 = ((f32[64,5,128]{2,1,0:T(8,128)}), f32[64,5,128]{2,1,0:T(8,128)S(1)}, u32[]{:S(2)}, u32[]{:S(2)}) async-start(f32[64,5,128]{2,1,0:T(8,128)} %broadcast_select_fusion.6), calls=%async_computation.1 | async-start | bytes 524288 | tf_op jit(solution)/shard_map/all_to_all | solution.py:107
where the time goes:
time: 256 us
  matrix products  147 us (57%)
  blocking collectives  45.1 us (18%)
  waiting for transfers between devices  20.6 us (8%)
  starting transfers between devices  18.2 us (7%)
  local copies, waits for them, and re-layouts  14.8 us (6%)
  other arithmetic  7.33 us (3%)
    dot_general x24, matrix products, tile_forces(): lax.dot_general(left_coords, right_coords, (((0,), (0,)), ((), ())), prec...  78.9 us
    dot_general x24, matrix products, tile_forces(): lax.dot_general(right_coords, coupling, (((1,), (1,)), ((), ())), precisi...  42.2 us
    all_to_all x2, blocking collectives, on_device(): lax.all_to_all(ghost_forces, 'dom', split_axis=0, concat_axis=0, tiled=True)  30.3 us
    dot_general x24, matrix products, tile_forces(): jnp.dot(left_coords, coupling, precision=highest, preferred_element_type=...  23.7 us
    all_to_all x1, blocking collectives, on_device(): lax.all_to_all(jnp.take(coords, send_rows, axis=0), 'dom', split_axis=0,...  14.8 us
    all_to_all x1, starting transfers between devices, on_device(): lax.all_to_all(outbound, 'dom', split_axis=0, concat_axis=0, tiled=True)  12.2 us
    all_to_all x1, waiting for transfers between devices, on_device(): lax.all_to_all(outgoing, 'dom', split_axis=0, concat_axis=0, tiled=True)  11.1 us
    all_to_all x1, waiting for transfers between devices, on_device(): lax.all_to_all(outbound, 'dom', split_axis=0, concat_axis=0, tiled=True)  9.5 us
  transfers between devices with their start and end apart: 2, of which 2 were waited for; matrix products, arithmetic and copies ran while one was open for 0% of the time, Pallas kernels for 0%

commit v1 on v0

v1 whole, which is shorter than its diff:
```python
import math

import jax
import jax.numpy as jnp
from jax import lax
from jax.experimental import pallas as pl
from jax.experimental.pallas import tpu as pltpu
from jax.sharding import PartitionSpec as P

BLOCK = 128
BLOCKS = 64
DOMAINS = 64
LOCAL = 128
GHOST = 64

coupling_scale = 0.2
time_step = 0.05
root_log2e = math.sqrt(math.log2(math.e))
local_unroll = 32
ghost_unroll = 16
f32 = jnp.float32
bf16 = jnp.bfloat16

vmem = pl.BlockSpec(memory_space=pltpu.VMEM)
smem = pl.BlockSpec(memory_space=pltpu.SMEM)


def rounded(values):
    return values.astype(bf16).astype(f32)


def split3(values):
    first = rounded(values)
    rest = values - first
    second = rounded(rest)
    return first, second, rounded(rest - second)


def exponent_parts(coords):
    scaled = coords * root_log2e
    half = 0.5 * jnp.sum(scaled * scaled, 0, keepdims=True)
    return split3(jnp.concatenate([scaled, half, scaled, half], 0))


def row_masks():
    row = lax.broadcasted_iota(jnp.int32, (8, BLOCK), 0)
    return row == 3, row == 7, row < 4


def source_rows(parts, charge):
    p0, p1, p2 = parts
    third, last, low = row_masks()
    s0 = jnp.where(third, -p0, jnp.where(last, -p1, p0))
    s1 = jnp.where(third, -p2, jnp.where(last, 1.0, p1))
    s2 = jnp.where(third | last, 1.0, jnp.where(low, p0, p2))
    return jnp.concatenate([s0, s1, s2, jnp.broadcast_to(charge, (8, BLOCK))], 0)


def target_rows(parts):
    p0, p1, p2 = parts
    third, last, low = row_masks()
    t0 = jnp.where(third | last, 1.0, jnp.where(low, p0, p1))
    t1 = jnp.where(third, 1.0, jnp.where(last, -p0, jnp.where(low, p0, p1)))
    t2 = jnp.where(third, -p1, jnp.where(last, -p2, jnp.where(low, p2, p0)))
    return jnp.concatenate([t0, t1, t2, jnp.zeros((8, BLOCK), f32)], 0).astype(bf16)


def weight_rows(coords, weight):
    low = row_masks()[2]
    ones = jnp.ones((1, BLOCK), f32)
    w0, w1, w2 = split3(jnp.concatenate([coords, ones, coords, ones], 0) * weight)
    return jnp.concatenate([jnp.where(low, w0, w1), jnp.where(low, w2, 0.0)], 0).astype(bf16)


def coupled_sums(sources, charges, weights, targets, target_charges):
    empty = jnp.zeros((32, BLOCK), bf16)
    right = jnp.concatenate(
        [
            jnp.concatenate([targets[0], empty], 1),
            jnp.concatenate([empty, targets[1]], 1),
        ],
        0,
    )
    exponent = jnp.dot(sources, right, preferred_element_type=f32)
    tiles = []
    for which in range(2):
        decay = jnp.exp2(exponent[:, which * BLOCK : (which + 1) * BLOCK])
        tiles.append(decay * (charges[which] * target_charges[which] + decay))
    coupling = jnp.concatenate(tiles, 1)
    high = coupling.astype(bf16)
    low = (coupling - high.astype(f32)).astype(bf16)
    stacked = jnp.concatenate([high, low], 0)
    left = jnp.concatenate(weights, 0)
    left = jnp.concatenate([left, left], 1)
    return jnp.dot(left, stacked, preferred_element_type=f32)


def pack_kernel(scale, send, positions, velocities, charges, solute, states, outbound):
    root = jnp.sqrt(jnp.full((8, BLOCK), scale[0], f32))

    def gather(group, carry):
        first = pl.multiple_of(group * 8, 8)
        charge_rows = charges[pl.ds(first, 8), :]
        weight = jnp.where(solute[pl.ds(first, 8), :] == 1, root, 1.0)
        for inner in range(8):
            lanes = pl.ds(pl.multiple_of((group * 8 + inner) * BLOCK, BLOCK), BLOCK)
            states[group * 8 + inner] = jnp.concatenate(
                [
                    positions[:, lanes],
                    velocities[:, lanes],
                    charge_rows[inner : inner + 1],
                    weight[inner : inner + 1],
                ],
                0,
            )
        return carry

    lax.fori_loop(0, BLOCKS // 8, gather, 0)

    def hand_over(group, carry):
        for inner in range(8):
            peer = group * 8 + inner
            outbound[peer] = states[jnp.minimum(send[0, peer], BLOCKS - 1)]
        return carry

    lax.fori_loop(0, DOMAINS // 8, hand_over, 0)


def home_table(home, other, homes):
    def enter(entry, carry):
        homes[other[0, LOCAL + entry] - BLOCKS] = home[0, LOCAL + entry]
        return carry

    lax.fori_loop(0, GHOST, enter, 0)


def place_kernel(land, ghost, home, other, states, arrived, placed, outgoing, homes):
    home_table(home, other, homes)

    def keep(group, carry):
        placed[pl.ds(group * 8, 8)] = states[pl.ds(group * 8, 8)]
        return carry

    lax.fori_loop(0, BLOCKS // 8, keep, 0)

    def receive(group, carry):
        for inner in range(8):
            peer = group * 8 + inner
            placed[land[0, peer]] = arrived[peer]
        return carry

    lax.fori_loop(0, DOMAINS // 8, receive, 0)

    def send(group, carry):
        for inner in range(8):
            peer = group * 8 + inner
            for which, slot in enumerate((ghost[0, peer], homes[peer])):
                for column, row in enumerate((0, 1, 2, 6, 7)):
                    outgoing[peer, which : which + 1, column * BLOCK : (column + 1) * BLOCK] = (
                        placed[slot, row : row + 1, :]
                    )
        return carry

    lax.fori_loop(0, DOMAINS // 8, send, 0)


def local_kernel(home, other, placed, sums, targets, first, second, weights, spread):
    def prepare(group, carry):
        stacked = []
        for inner in range(4):
            block = group * 4 + inner
            state = placed[block]
            parts = exponent_parts(state[0:3])
            targets[block] = target_rows(parts)
            weights[block] = weight_rows(state[0:3], state[7:8])
            stacked.append(source_rows(parts, state[6:7]))
            sums[block] = jnp.zeros((16, BLOCK), f32)
        columns = jnp.concatenate(stacked, 0).T
        empty = jnp.zeros((BLOCK, 32), bf16)
        for inner in range(4):
            block = group * 4 + inner
            chosen = columns[:, inner * 32 : (inner + 1) * 32]
            narrow = chosen.astype(bf16)
            first[block] = jnp.concatenate([narrow, empty], 1)
            second[block] = jnp.concatenate([empty, narrow], 1)
            spread[block] = jnp.broadcast_to(chosen[:, 24:25], (BLOCK, BLOCK))
        return carry

    lax.fori_loop(0, BLOCKS // 4, prepare, 0)

    def pairs(group, carry):
        for inner in range(local_unroll):
            entry = group * local_unroll + inner
            one = home[0, entry]
            two = other[0, entry]
            result = coupled_sums(
                first[two] + second[one],
                (spread[two], spread[one]),
                (weights[two], weights[one]),
                (targets[one], targets[two]),
                (placed[one, 6:7, :], placed[two, 6:7, :]),
            )
            sums[one] += result[:16, :BLOCK]
            sums[two] += result[16:, BLOCK:]
        return carry

    lax.fori_loop(0, LOCAL // local_unroll, pairs, 0)


def ghost_pairs(ghost, homes, placed, targets, sums, total, coords_of, params_of):
    def start(group, carry):
        total[pl.ds(group * 8, 8)] = sums[pl.ds(group * 8, 8)]
        return carry

    lax.fori_loop(0, BLOCKS // 8, start, 0)

    def pairs(group, carry):
        for half in range(ghost_unroll // 2):
            stacked = []
            weights = []
            for inner in range(2):
                peer = group * ghost_unroll + half * 2 + inner
                for which in range(2):
                    coords = coords_of(peer, which)
                    charge, weight = params_of(peer, which)
                    stacked.append(source_rows(exponent_parts(coords), charge))
                    weights.append(weight_rows(coords, weight))
            columns = jnp.concatenate(stacked, 0).T
            narrow = columns.astype(bf16)
            for inner in range(2):
                peer = group * ghost_unroll + half * 2 + inner
                one = homes[peer]
                two = ghost[0, peer]
                lane = inner * 64
                result = coupled_sums(
                    narrow[:, lane : lane + 64],
                    (
                        jnp.broadcast_to(columns[:, lane + 24 : lane + 25], (BLOCK, BLOCK)),
                        jnp.broadcast_to(columns[:, lane + 56 : lane + 57], (BLOCK, BLOCK)),
                    ),
                    (weights[inner * 2], weights[inner * 2 + 1]),
                    (targets[one], targets[two]),
                    (placed[one, 6:7, :], placed[two, 6:7, :]),
                )
                total[one] += result[:16, :BLOCK]
                total[two] += result[16:, BLOCK:]
        return carry

    lax.fori_loop(0, DOMAINS // ghost_unroll, pairs, 0)


def moved(state, total):
    folded = total[0:4] + total[4:8] + total[8:12]
    force = (coupling_scale * state[7:8]) * (state[0:3] * folded[3:4] - folded[0:3])
    speed = state[3:6] + time_step * force
    return state[0:3] + time_step * speed, speed, force


def middle_kernel(
    ghost, home, other, placed, sums, targets, received, updated, outgoing, homes, total
):
    home_table(home, other, homes)

    def row(peer, which, column):
        return received[peer, which : which + 1, column * BLOCK : (column + 1) * BLOCK]

    ghost_pairs(
        ghost,
        homes,
        placed,
        targets,
        sums,
        total,
        lambda peer, which: jnp.concatenate([row(peer, which, c) for c in range(3)], 0),
        lambda peer, which: (row(peer, which, 3), row(peer, which, 4)),
    )

    def step(group, carry):
        for inner in range(8):
            block = group * 8 + inner
            state = placed[block]
            coords, speed, _ = moved(state, total[block])
            updated[block] = jnp.concatenate([coords, speed, state[6:8]], 0)
        return carry

    lax.fori_loop(0, BLOCKS // 8, step, 0)

    def send(group, carry):
        for inner in range(8):
            peer = group * 8 + inner
            for which, slot in enumerate((ghost[0, peer], homes[peer])):
                for column in range(3):
                    outgoing[peer, which : which + 1, column * BLOCK : (column + 1) * BLOCK] = (
                        updated[slot, column : column + 1, :]
                    )
        return carry

    lax.fori_loop(0, DOMAINS // 8, send, 0)


def last_kernel(
    ghost,
    home,
    other,
    placed,
    sums,
    targets,
    received,
    earlier,
    coords_out,
    speeds_out,
    forces_out,
    homes,
    total,
):
    home_table(home, other, homes)

    def row(ref, peer, which, column):
        return ref[peer, which : which + 1, column * BLOCK : (column + 1) * BLOCK]

    ghost_pairs(
        ghost,
        homes,
        placed,
        targets,
        sums,
        total,
        lambda peer, which: jnp.concatenate([row(received, peer, which, c) for c in range(3)], 0),
        lambda peer, which: (row(earlier, peer, which, 3), row(earlier, peer, which, 4)),
    )

    def step(group, carry):
        for inner in range(8):
            block = group * 8 + inner
            coords, speed, force = moved(placed[block], total[block])
            lanes = pl.ds(pl.multiple_of(block * BLOCK, BLOCK), BLOCK)
            coords_out[:, lanes] = coords
            speeds_out[:, lanes] = speed
            forces_out[:, lanes] = force
        return carry

    lax.fori_loop(0, BLOCKS // 8, step, 0)


def shape(*dims, dtype=f32):
    return jax.ShapeDtypeStruct(dims, dtype)


def pack(scale, send, positions, velocities, charges, solute):
    return pl.pallas_call(
        pack_kernel,
        in_specs=[smem, smem, vmem, vmem, vmem, vmem],
        out_specs=(vmem, vmem),
        out_shape=(shape(BLOCKS, 8, BLOCK), shape(DOMAINS, 8, BLOCK)),
    )(scale, send, positions, velocities, charges, solute)


def place(land, ghost, home, other, states, arrived):
    return pl.pallas_call(
        place_kernel,
        in_specs=[smem, smem, smem, smem, vmem, vmem],
        out_specs=(vmem, vmem),
        out_shape=(shape(BLOCKS + 1, 8, BLOCK), shape(DOMAINS, 2, 5 * BLOCK)),
        scratch_shapes=[pltpu.SMEM((DOMAINS,), jnp.int32)],
    )(land, ghost, home, other, states, arrived)


def local_pairs(home, other, placed):
    return pl.pallas_call(
        local_kernel,
        in_specs=[smem, smem, vmem],
        out_specs=(vmem, vmem),
        out_shape=(shape(BLOCKS, 16, BLOCK), shape(BLOCKS, 32, BLOCK, dtype=bf16)),
        scratch_shapes=[
            pltpu.VMEM((BLOCKS, BLOCK, 64), bf16),
            pltpu.VMEM((BLOCKS, BLOCK, 64), bf16),
            pltpu.VMEM((BLOCKS, 16, BLOCK), bf16),
            pltpu.VMEM((BLOCKS, BLOCK, BLOCK), f32),
        ],
        cost_estimate=pl.CostEstimate(
            flops=1_000_000_000, transcendentals=4_000_000, bytes_accessed=1_000_000
        ),
    )(home, other, placed)


def middle(ghost, home, other, placed, sums, targets, received):
    return pl.pallas_call(
        middle_kernel,
        in_specs=[smem, smem, smem, vmem, vmem, vmem, vmem],
        out_specs=(vmem, vmem),
        out_shape=(shape(BLOCKS + 1, 8, BLOCK), shape(DOMAINS, 2, 3 * BLOCK)),
        scratch_shapes=[
            pltpu.SMEM((DOMAINS,), jnp.int32),
            pltpu.VMEM((BLOCKS, 16, BLOCK), f32),
        ],
    )(ghost, home, other, placed, sums, targets, received)


def last(ghost, home, other, placed, sums, targets, received, earlier):
    flat = shape(3, BLOCKS * BLOCK)
    return pl.pallas_call(
        last_kernel,
        in_specs=[smem, smem, smem, vmem, vmem, vmem, vmem, vmem],
        out_specs=(vmem, vmem, vmem),
        out_shape=(flat, flat, flat),
        scratch_shapes=[
            pltpu.SMEM((DOMAINS,), jnp.int32),
            pltpu.VMEM((BLOCKS, 16, BLOCK), f32),
        ],
    )(ghost, home, other, placed, sums, targets, received, earlier)


def exchange(values):
    return lax.all_to_all(values, "dom", split_axis=0, concat_axis=0, tiled=True)


def on_device(
    positions,
    velocities,
    charges,
    solute,
    rest_scale,
    send_slot,
    land_slot,
    ghost_slot,
    pair_home,
    pair_other,
):
    states, outbound = pack(
        rest_scale,
        send_slot,
        positions,
        velocities,
        charges.reshape(BLOCKS, BLOCK),
        solute.reshape(BLOCKS, BLOCK),
    )
    arrived = exchange(outbound)
    placed, outgoing = place(land_slot, ghost_slot, pair_home, pair_other, states, arrived)
    ghosts = exchange(outgoing)
    sums, targets = local_pairs(pair_home, pair_other, placed)
    placed, outgoing = middle(ghost_slot, pair_home, pair_other, placed, sums, targets, ghosts)
    moved_ghosts = exchange(outgoing)
    sums, targets = local_pairs(pair_home, pair_other, placed)
    return last(
        ghost_slot, pair_home, pair_other, placed, sums, targets, moved_ghosts, ghosts
    )


def solution(mesh):
    in_specs = (
        P(None, ("rep", "dom")),
        P(None, ("rep", "dom")),
        P(("rep", "dom")),
        P(("rep", "dom")),
        P("rep"),
        P(("rep", "dom"), None),
        P(("rep", "dom"), None),
        P(("rep", "dom"), None),
        P(("rep", "dom"), None),
        P(("rep", "dom"), None),
    )
    out_specs = (P(None, ("rep", "dom")), P(None, ("rep", "dom")), P(None, ("rep", "dom")))
    return jax.shard_map(
        on_device, mesh=mesh, in_specs=in_specs, out_specs=out_specs, check_vma=False
    )
```

time: 256 us -> 89.8 us (0.35)
  matrix products: 147 us -> 0 us
  Pallas kernels: 0 us -> 46.1 us
  blocking collectives: 45.1 us -> 23.8 us
  waiting for transfers between devices: 20.6 us -> 0.01 us
  local copies, waits for them, and re-layouts: 14.8 us -> 1.41 us
  other arithmetic: 7.33 us -> 0 us
    dot_general x78 -> x0, matrix products: 147 us -> none  [the longest x24 78.9 us: tile_forces(): lax.dot_general(left_coords, right_coords, (((0,), (0,)), ((), ())), prec...]
    pallas_call x0 -> x6, Pallas kernels: none -> 46.1 us  [the longest x2 25.3 us: local_pairs(): pl.pallas_call(local_kernel, in_specs=[smem, smem, vmem], out_specs=(vmem...]
    all_to_all x3 -> x1, blocking collectives: 45.1 us -> 23.8 us  [exchange(): lax.all_to_all(values, 'dom', split_axis=0, concat_axis=0, tiled=True)]
    all_to_all x2, waiting for transfers between devices: 20.6 us -> 0.01 us  [exchange(): lax.all_to_all(values, 'dom', split_axis=0, concat_axis=0, tiled=True)]
    gather x9 -> x0, local copies, waits for them, and re-layouts: 7.14 us -> none  [the longest x2 1.75 us: on_device(): jnp.take(table_coords, home_rows, axis=0)]
    select_n x14 -> x0, other arithmetic: 4.12 us -> none  [the longest x2 1.54 us: on_device(): outbound = jnp.take(padded, send_slot[0], axis=0)]
  transfers between devices with their start and end apart: 2 -> 2, of which waited for: 2 -> 0; matrix products, arithmetic and copies ran while one was open for 0% -> 0% of each run, Pallas kernels for 0% -> 28%
where the time goes in v1:
time: 89.8 us; the launch traced here: 89.3 us
  Pallas kernels  46.1 us (51%)
  blocking collectives  23.8 us (27%)
  starting transfers between devices  16.8 us (19%)
  local copies, waits for them, and re-layouts  1.41 us (2%)
  between operations  1.31 us (1%)
    pallas_call x2, Pallas kernels, local_pairs(): pl.pallas_call(local_kernel, in_specs=[smem, smem, vmem], out_specs=(vmem...  25.3 us
    all_to_all x1, blocking collectives, exchange(): lax.all_to_all(values, 'dom', split_axis=0, concat_axis=0, tiled=True)  23.8 us
    all_to_all x2, starting transfers between devices, exchange(): lax.all_to_all(values, 'dom', split_axis=0, concat_axis=0, tiled=True)  16.8 us
    pallas_call x1, Pallas kernels, middle(): pl.pallas_call(middle_kernel, in_specs=[smem, smem, smem, vmem, vmem, vme...  8.07 us
    pallas_call x1, Pallas kernels, last(): pl.pallas_call(last_kernel, in_specs=[smem, smem, smem, vmem, vmem, vmem,...  7.84 us
    pallas_call x1, Pallas kernels, place(): pl.pallas_call(place_kernel, in_specs=[smem, smem, smem, smem, vmem, vmem...  2.82 us
    pallas_call x1, Pallas kernels, pack(): pl.pallas_call(pack_kernel, in_specs=[smem, smem, vmem, vmem, vmem, vmem]...  2.05 us
  transfers between devices with their start and end apart: 2, of which 0 were waited for; matrix products, arithmetic and copies ran while one was open for 0% of the time, Pallas kernels for 28%

profile of v1, /device:TPU:2, one launch (start us, length us, event | category | flops | bytes accessed | tf_op | source)
XLA Modules:
  0.0 89.3 jit_solution(10134598568425927318)
XLA Ops:
  1.3 2.0 %shard_map.121 = (f32[64,8,128]{2,1,0:T(8,128)}, f32[64,8,128]{2,1,0:T(8,128)}) custom-call(f32[1]{0:T(128)S(6)} %copy.13.scale, s32[1,64]{1,0:T(1,128)} %send.1, f32[3,8192]{1,0:T(4,128)} %positions.1, f32[3,8192]{1,0:T(4,128)} %velocities.1, f32[64,128]{1,0:T(8,128)} %bitcast.2, s32[64,128]{1,0:T(8,128)} %bitcast.3), custom_call_target="tpu_custom_call" | custom-call | tf_op jit(solution)/shard_map/pallas_call | solution.py:350
  3.3 23.8 %all_to_all.15.arrived = f32[64,8,128]{2,1,0:T(8,128)} all-to-all(f32[64,8,128]{2,1,0:T(8,128)} %get-tuple-element.14), channel_id=1, replica_groups=mesh['rep'=4,'dom'=64] {'dom'}, dimensions={0} | all-to-all | bytes 524288 | tf_op jit(solution)/shard_map/all_to_all | solution.py:414
  27.1 2.8 %shard_map.122 = (f32[65,8,128]{2,1,0:T(8,128)}, f32[64,2,640]{2,1,0:T(2,128)}) custom-call(s32[1,64]{1,0:T(1,128)} %land.1, s32[1,64]{1,0:T(1,128)} %ghost.5, s32[1,192]{1,0:T(1,128)} %home.9, s32[1,192]{1,0:T(1,128)} %other.9, f32[64,8,128]{2,1,0:T(8,128)} %get-tuple-element.13.states, f32[64,8,128]{2,1,0:T(8,128)} %all_to_all.15.arrived), custom_call_target="tpu_custom_call" | custom-call | tf_op jit(solution)/shard_map/pallas_call | solution.py:359
  29.9 6.0 %all-to-all-start.1 = ((f32[64,2,640]{2,1,0:T(2,128)}), f32[64,2,640]{2,1,0:T(2,128)S(1)}, u32[]{:S(2)}, u32[]{:S(2)}) async-start(f32[64,2,640]{2,1,0:T(2,128)} %get-tuple-element.18), calls=%async_computation.1 | async-start | bytes 655360 | tf_op jit(solution)/shard_map/all_to_all | solution.py:414
  35.9 12.7 %shard_map.123 = (f32[64,16,128]{2,1,0:T(8,128)}, bf16[64,32,128]{2,1,0:T(8,128)(2,1)}) custom-call(s32[1,192]{1,0:T(1,128)} %home.9, s32[1,192]{1,0:T(1,128)} %other.9, f32[65,8,128]{2,1,0:T(8,128)} %get-tuple-element.15.placed), custom_call_target="tpu_custom_call" | custom-call | flops 1000000000 | bytes 1000000 | tf_op jit(solution)/shard_map/pallas_call | solution.py:369
  48.6 0.0 all-to-all-done.1.received.earlier
  48.6 0.0 copy-start
  48.6 0.7 copy-done
  49.3 8.1 %shard_map.124 = (f32[65,8,128]{2,1,0:T(8,128)}, f32[64,2,384]{2,1,0:T(2,128)}) custom-call(s32[1,64]{1,0:T(1,128)} %ghost.5, s32[1,192]{1,0:T(1,128)} %home.9, s32[1,192]{1,0:T(1,128)} %other.9, f32[65,8,128]{2,1,0:T(8,128)} %get-tuple-element.15.placed, f32[64,16,128]{2,1,0:T(8,128)} %get-tuple-element.16.sums, ...), custom_call_target="tpu_custom_call" | custom-call | tf_op jit(solution)/shard_map/pallas_call | solution.py:387
  57.4 10.8 %all-to-all-start.2 = ((f32[64,2,384]{2,1,0:T(2,128)}), f32[64,2,384]{2,1,0:T(2,128)S(1)}, u32[]{:S(2)}, u32[]{:S(2)}) async-start(f32[64,2,384]{2,1,0:T(2,128)} %get-tuple-element.22), calls=%async_computation.2 | async-start | bytes 393216 | tf_op jit(solution)/shard_map/all_to_all | solution.py:414
  68.2 12.6 %shard_map.125 = (f32[64,16,128]{2,1,0:T(8,128)}, bf16[64,32,128]{2,1,0:T(8,128)(2,1)}) custom-call(s32[1,192]{1,0:T(1,128)} %home.9, s32[1,192]{1,0:T(1,128)} %other.9, f32[65,8,128]{2,1,0:T(8,128)} %get-tuple-element.19.placed), custom_call_target="tpu_custom_call" | custom-call | flops 1000000000 | bytes 1000000 | tf_op jit(solution)/shard_map/pallas_call | solution.py:369
  80.8 0.0 all-to-all-done.2.received
  80.8 0.0 copy-start.1
  80.8 0.7 copy-done.1
  81.5 7.8 %shard_map.126 = (f32[3,8192]{1,0:T(4,128)}, f32[3,8192]{1,0:T(4,128)}, f32[3,8192]{1,0:T(4,128)}) custom-call(s32[1,64]{1,0:T(1,128)} %ghost.5, s32[1,192]{1,0:T(1,128)} %home.9, s32[1,192]{1,0:T(1,128)} %other.9, f32[65,8,128]{2,1,0:T(8,128)} %get-tuple-element.19.placed, f32[64,16,128]{2,1,0:T(8,128)} %get-tuple-element.20.sums, ...), custom_call_target="tpu_custom_call" | custom-call | tf_op jit(solution)/shard_map/pallas_call | solution.py:401
Async XLA Ops:
  29.9 18.7 %all-to-all-start.1 = ((f32[64,2,640]{2,1,0:T(2,128)}), f32[64,2,640]{2,1,0:T(2,128)S(1)}, u32[]{:S(2)}, u32[]{:S(2)}) async-start(f32[64,2,640]{2,1,0:T(2,128)} %get-tuple-element.18), calls=%async_computation.1 | async-start | bytes 655360 | tf_op jit(solution)/shard_map/all_to_all | solution.py:414
  48.6 0.7 copy-start
  57.4 23.4 %all-to-all-start.2 = ((f32[64,2,384]{2,1,0:T(2,128)}), f32[64,2,384]{2,1,0:T(2,128)S(1)}, u32[]{:S(2)}, u32[]{:S(2)}) async-start(f32[64,2,384]{2,1,0:T(2,128)} %get-tuple-element.22), calls=%async_computation.2 | async-start | bytes 393216 | tf_op jit(solution)/shard_map/all_to_all | solution.py:414
  80.8 0.7 copy-start.1

commit v2 on v1

--- a/solution.py
+++ b/solution.py
@@ -11,13 +11,13 @@
 BLOCKS = 64
 DOMAINS = 64
 LOCAL = 128
-GHOST = 64
+LAND, SENT, MATE, HOME, OTHER = range(5)
 
 coupling_scale = 0.2
 time_step = 0.05
 root_log2e = math.sqrt(math.log2(math.e))
 local_unroll = 32
-ghost_unroll = 16
+ghost_unroll = 32
 f32 = jnp.float32
 bf16 = jnp.bfloat16
 
@@ -126,17 +126,24 @@
     lax.fori_loop(0, DOMAINS // 8, hand_over, 0)
 
 
-def home_table(home, other, homes):
-    def enter(entry, carry):
-        homes[other[0, LOCAL + entry] - BLOCKS] = home[0, LOCAL + entry]
-        return carry
-
-    lax.fori_loop(0, GHOST, enter, 0)
-
-
-def place_kernel(land, ghost, home, other, states, arrived, placed, outgoing, homes):
-    home_table(home, other, homes)
-
+def table_kernel(land, ghost, home, other, table):
+    def by_peer(peer, carry):
+        table[LAND, peer] = land[0, peer]
+        table[SENT, peer] = ghost[0, peer]
+        table[MATE, other[0, LOCAL + peer] - BLOCKS] = home[0, LOCAL + peer]
+        return carry
+
+    lax.fori_loop(0, DOMAINS, by_peer, 0)
+
+    def by_pair(entry, carry):
+        table[HOME, entry] = home[0, entry]
+        table[OTHER, entry] = other[0, entry]
+        return carry
+
+    lax.fori_loop(0, LOCAL, by_pair, 0)
+
+
+def place_kernel(table, states, arrived, placed, outgoing):
     def keep(group, carry):
         placed[pl.ds(group * 8, 8)] = states[pl.ds(group * 8, 8)]
         return carry
@@ -146,7 +153,7 @@
     def receive(group, carry):
         for inner in range(8):
             peer = group * 8 + inner
-            placed[land[0, peer]] = arrived[peer]
+            placed[table[LAND, peer]] = arrived[peer]
         return carry
 
     lax.fori_loop(0, DOMAINS // 8, receive, 0)
@@ -154,7 +161,7 @@
     def send(group, carry):
         for inner in range(8):
             peer = group * 8 + inner
-            for which, slot in enumerate((ghost[0, peer], homes[peer])):
+            for which, slot in enumerate((table[SENT, peer], table[MATE, peer])):
                 for column, row in enumerate((0, 1, 2, 6, 7)):
                     outgoing[peer, which : which + 1, column * BLOCK : (column + 1) * BLOCK] = (
                         placed[slot, row : row + 1, :]
@@ -164,8 +171,8 @@
     lax.fori_loop(0, DOMAINS // 8, send, 0)
 
 
-def local_kernel(home, other, placed, sums, targets, first, second, weights, spread):
-    def prepare(group, carry):
+def local_kernel(table, placed, sums, targets, first, second, weights, spread):
+    def prepare(group):
         stacked = []
         for inner in range(4):
             block = group * 4 + inner
@@ -184,15 +191,19 @@
             first[block] = jnp.concatenate([narrow, empty], 1)
             second[block] = jnp.concatenate([empty, narrow], 1)
             spread[block] = jnp.broadcast_to(chosen[:, 24:25], (BLOCK, BLOCK))
-        return carry
-
-    lax.fori_loop(0, BLOCKS // 4, prepare, 0)
+
+    def prepare_some(chunk, carry):
+        for inner in range(4):
+            prepare(chunk * 4 + inner)
+        return carry
+
+    lax.fori_loop(0, BLOCKS // 16, prepare_some, 0)
 
     def pairs(group, carry):
         for inner in range(local_unroll):
             entry = group * local_unroll + inner
-            one = home[0, entry]
-            two = other[0, entry]
+            one = table[HOME, entry]
+            two = table[OTHER, entry]
             result = coupled_sums(
                 first[two] + second[one],
                 (spread[two], spread[one]),
@@ -207,7 +218,7 @@
     lax.fori_loop(0, LOCAL // local_unroll, pairs, 0)
 
 
-def ghost_pairs(ghost, homes, placed, targets, sums, total, coords_of, params_of):
+def ghost_pairs(table, placed, targets, sums, total, coords_of, params_of):
     def start(group, carry):
         total[pl.ds(group * 8, 8)] = sums[pl.ds(group * 8, 8)]
         return carry
@@ -229,8 +240,8 @@
             narrow = columns.astype(bf16)
             for inner in range(2):
                 peer = group * ghost_unroll + half * 2 + inner
-                one = homes[peer]
-                two = ghost[0, peer]
+                one = table[MATE, peer]
+                two = table[SENT, peer]
                 lane = inner * 64
                 result = coupled_sums(
                     narrow[:, lane : lane + 64],
@@ -256,17 +267,12 @@
     return state[0:3] + time_step * speed, speed, force
 
 
-def middle_kernel(
-    ghost, home, other, placed, sums, targets, received, updated, outgoing, homes, total
-):
-    home_table(home, other, homes)
-
+def middle_kernel(table, placed, sums, targets, received, updated, outgoing, total):
     def row(peer, which, column):
         return received[peer, which : which + 1, column * BLOCK : (column + 1) * BLOCK]
 
     ghost_pairs(
-        ghost,
-        homes,
+        table,
         placed,
         targets,
         sums,
@@ -288,7 +294,7 @@
     def send(group, carry):
         for inner in range(8):
             peer = group * 8 + inner
-            for which, slot in enumerate((ghost[0, peer], homes[peer])):
+            for which, slot in enumerate((table[SENT, peer], table[MATE, peer])):
                 for column in range(3):
                     outgoing[peer, which : which + 1, column * BLOCK : (column + 1) * BLOCK] = (
                         updated[slot, column : column + 1, :]
@@ -299,9 +305,7 @@
 
 
 def last_kernel(
-    ghost,
-    home,
-    other,
+    table,
     placed,
     sums,
     targets,
@@ -310,17 +314,13 @@
     coords_out,
     speeds_out,
     forces_out,
-    homes,
     total,
 ):
-    home_table(home, other, homes)
-
     def row(ref, peer, which, column):
         return ref[peer, which : which + 1, column * BLOCK : (column + 1) * BLOCK]
 
     ghost_pairs(
-        ghost,
-        homes,
+        table,
         placed,
         targets,
         sums,
@@ -342,33 +342,56 @@
     lax.fori_loop(0, BLOCKS // 8, step, 0)
 
 
+def grant(mebibytes):
+    return pltpu.CompilerParams(vmem_limit_bytes=mebibytes << 20)
+
+
 def shape(*dims, dtype=f32):
     return jax.ShapeDtypeStruct(dims, dtype)
 
 
+def in_hbm(values):
+    return pltpu.with_memory_space_constraint(values, pltpu.HBM)
+
+
 def pack(scale, send, positions, velocities, charges, solute):
     return pl.pallas_call(
         pack_kernel,
+        compiler_params=grant(4),
         in_specs=[smem, smem, vmem, vmem, vmem, vmem],
         out_specs=(vmem, vmem),
         out_shape=(shape(BLOCKS, 8, BLOCK), shape(DOMAINS, 8, BLOCK)),
-    )(scale, send, positions, velocities, charges, solute)
-
-
-def place(land, ghost, home, other, states, arrived):
+    )(scale, send, *(in_hbm(x) for x in (positions, velocities, charges, solute)))
+
+
+def tables(land, ghost, home, other):
+    return pl.pallas_call(
+        table_kernel,
+        compiler_params=grant(1),
+        in_specs=[smem, smem, smem, smem],
+        out_specs=smem,
+        out_shape=shape(8, LOCAL, dtype=jnp.int32),
+        cost_estimate=pl.CostEstimate(
+            flops=100_000_000, transcendentals=0, bytes_accessed=10_000
+        ),
+    )(land, ghost, home, other)
+
+
+def place(table, states, arrived):
     return pl.pallas_call(
         place_kernel,
-        in_specs=[smem, smem, smem, smem, vmem, vmem],
+        compiler_params=grant(4),
+        in_specs=[smem, vmem, vmem],
         out_specs=(vmem, vmem),
         out_shape=(shape(BLOCKS + 1, 8, BLOCK), shape(DOMAINS, 2, 5 * BLOCK)),
-        scratch_shapes=[pltpu.SMEM((DOMAINS,), jnp.int32)],
-    )(land, ghost, home, other, states, arrived)
-
-
-def local_pairs(home, other, placed):
+    )(table, states, arrived)
+
+
+def local_pairs(table, placed):
     return pl.pallas_call(
         local_kernel,
-        in_specs=[smem, smem, vmem],
+        compiler_params=grant(16),
+        in_specs=[smem, vmem],
         out_specs=(vmem, vmem),
         out_shape=(shape(BLOCKS, 16, BLOCK), shape(BLOCKS, 32, BLOCK, dtype=bf16)),
         scratch_shapes=[
@@ -380,34 +403,34 @@
         cost_estimate=pl.CostEstimate(
             flops=1_000_000_000, transcendentals=4_000_000, bytes_accessed=1_000_000
         ),
-    )(home, other, placed)
-
-
-def middle(ghost, home, other, placed, sums, targets, received):
+    )(table, placed)
+
+
+def middle(table, placed, sums, targets, received):
     return pl.pallas_call(
         middle_kernel,
-        in_specs=[smem, smem, smem, vmem, vmem, vmem, vmem],
+        compiler_params=grant(8),
+        in_specs=[smem, vmem, vmem, vmem, vmem],
         out_specs=(vmem, vmem),
         out_shape=(shape(BLOCKS + 1, 8, BLOCK), shape(DOMAINS, 2, 3 * BLOCK)),
         scratch_shapes=[
-            pltpu.SMEM((DOMAINS,), jnp.int32),
             pltpu.VMEM((BLOCKS, 16, BLOCK), f32),
         ],
-    )(ghost, home, other, placed, sums, targets, received)
-
-
-def last(ghost, home, other, placed, sums, targets, received, earlier):
+    )(table, placed, sums, targets, received)
+
+
+def last(table, placed, sums, targets, received, earlier):
     flat = shape(3, BLOCKS * BLOCK)
     return pl.pallas_call(
         last_kernel,
-        in_specs=[smem, smem, smem, vmem, vmem, vmem, vmem, vmem],
+        compiler_params=grant(8),
+        in_specs=[smem, vmem, vmem, vmem, vmem, vmem],
         out_specs=(vmem, vmem, vmem),
         out_shape=(flat, flat, flat),
         scratch_shapes=[
-            pltpu.SMEM((DOMAINS,), jnp.int32),
             pltpu.VMEM((BLOCKS, 16, BLOCK), f32),
         ],
-    )(ghost, home, other, placed, sums, targets, received, earlier)
+    )(table, placed, sums, targets, received, earlier)
 
 
 def exchange(values):
@@ -435,15 +458,14 @@
         solute.reshape(BLOCKS, BLOCK),
     )
     arrived = exchange(outbound)
-    placed, outgoing = place(land_slot, ghost_slot, pair_home, pair_other, states, arrived)
+    table = tables(land_slot, ghost_slot, pair_home, pair_other)
+    placed, outgoing = place(table, states, arrived)
     ghosts = exchange(outgoing)
-    sums, targets = local_pairs(pair_home, pair_other, placed)
-    placed, outgoing = middle(ghost_slot, pair_home, pair_other, placed, sums, targets, ghosts)
+    sums, targets = local_pairs(table, placed)
+    placed, outgoing = middle(table, placed, sums, targets, ghosts)
     moved_ghosts = exchange(outgoing)
-    sums, targets = local_pairs(pair_home, pair_other, placed)
-    return last(
-        ghost_slot, pair_home, pair_other, placed, sums, targets, moved_ghosts, ghosts
-    )
+    sums, targets = local_pairs(table, placed)
+    return last(table, placed, sums, targets, moved_ghosts, ghosts)
 
 
 def solution(mesh):

time: 89.8 us -> 77.9 us (0.87)
  blocking collectives: 23.8 us -> 0 us
  waiting for transfers between devices: 0.01 us -> 14 us
  Pallas kernels: 46.1 us -> 36.2 us
  starting transfers between devices: 16.8 us -> 25.3 us
    all_to_all x1 -> x0, blocking collectives: 23.8 us -> none  [exchange(): lax.all_to_all(values, 'dom', split_axis=0, concat_axis=0, tiled=True)]
    all_to_all x2 -> x3, waiting for transfers between devices: 0.01 us -> 14 us  [exchange(): lax.all_to_all(values, 'dom', split_axis=0, concat_axis=0, tiled=True)]
    pallas_call x6 -> x7, Pallas kernels: 46.1 us -> 36.2 us  [the longest x2 17.5 us: local_pairs(): pl.pallas_call(local_kernel, compiler_params=grant(16), in_specs=[smem, v...]
    all_to_all x2 -> x3, starting transfers between devices: 16.8 us -> 25.3 us  [exchange(): lax.all_to_all(values, 'dom', split_axis=0, concat_axis=0, tiled=True)]
  transfers between devices with their start and end apart: 2 -> 3, of which waited for: 0 -> 3; matrix products, arithmetic and copies ran while one was open for 0% -> 0% of each run, Pallas kernels for 28% -> 26%
where the time goes in v2:
time: 77.9 us; the launch traced here: 77.5 us
  Pallas kernels  36.2 us (46%)
  starting transfers between devices  25.3 us (32%)
  waiting for transfers between devices  14 us (18%)
  between operations  1.37 us (2%)
    all_to_all x3, starting transfers between devices, exchange(): lax.all_to_all(values, 'dom', split_axis=0, concat_axis=0, tiled=True)  25.3 us
    pallas_call x2, Pallas kernels, local_pairs(): pl.pallas_call(local_kernel, compiler_params=grant(16), in_specs=[smem, v...  17.5 us
    all_to_all x3, waiting for transfers between devices, exchange(): lax.all_to_all(values, 'dom', split_axis=0, concat_axis=0, tiled=True)  14 us
    pallas_call x1, Pallas kernels, middle(): pl.pallas_call(middle_kernel, compiler_params=grant(8), in_specs=[smem, v...  6.12 us
    pallas_call x1, Pallas kernels, last(): pl.pallas_call(last_kernel, compiler_params=grant(8), in_specs=[smem, vme...  5.85 us
    pallas_call x1, Pallas kernels, tables(): pl.pallas_call(table_kernel, compiler_params=grant(1), in_specs=[smem, sm...  2.81 us
    pallas_call x1, Pallas kernels, place(): pl.pallas_call(place_kernel, compiler_params=grant(4), in_specs=[smem, vm...  1.96 us
    pallas_call x1, Pallas kernels, pack(): pl.pallas_call(pack_kernel, compiler_params=grant(4), in_specs=[smem, sme...  1.96 us
  transfers between devices with their start and end apart: 3, of which 3 were waited for; matrix products, arithmetic and copies ran while one was open for 0% of the time, Pallas kernels for 26%

profile of v2, /device:TPU:2, one launch (start us, length us, event | category | flops | bytes accessed | tf_op | source)
XLA Modules:
  0.0 77.5 jit_solution(4741394210720401102)
XLA Ops:
  1.3 0.0 copy-start
  1.3 0.6 copy-done
  1.9 2.0 %shard_map.122 = (f32[64,8,128]{2,1,0:T(8,128)S(1)}, f32[64,8,128]{2,1,0:T(8,128)}) custom-call(f32[1]{0:T(128)S(6)} %copy.13.scale, s32[1,64]{1,0:T(1,128)S(1)} %copy-done, f32[3,8192]{1,0:T(4,128)} %positions.1, f32[3,8192]{1,0:T(4,128)} %velocities.1, f32[64,128]{1,0:T(8,128)} %bitcast.2, s32[64,128]{1,0:T(8,128)} %bitcast.3), custom_call_target="tpu_custom_call" | custom-call | tf_op jit(solution)/shard_map/pallas_call | solution.py:358
  3.9 0.0 copy-start.1
  3.9 0.0 copy-start.2
  3.9 0.0 copy-start.3
  3.9 0.0 copy-start.4
  3.9 12.2 %all-to-all-start = ((f32[64,8,128]{2,1,0:T(8,128)}), f32[64,8,128]{2,1,0:T(8,128)S(1)}, u32[]{:S(2)}, u32[]{:S(2)}) async-start(f32[64,8,128]{2,1,0:T(8,128)} %get-tuple-element.14), calls=%async_computation | async-start | bytes 524288 | tf_op jit(solution)/shard_map/all_to_all | solution.py:437
  16.2 0.0 copy-done.1
  16.2 0.0 copy-done.2
  16.2 0.0 copy-done.3
  16.2 0.0 copy-done.4
  16.2 2.8 %shard_map.121.table = s32[8,128]{1,0:T(8,128)S(1)} custom-call(s32[1,64]{1,0:T(1,128)S(1)} %copy-done.3, s32[1,64]{1,0:T(1,128)S(1)} %copy-done.4, s32[1,192]{1,0:T(1,128)S(1)} %copy-done.1, s32[1,192]{1,0:T(1,128)S(1)} %copy-done.2), custom_call_target="tpu_custom_call" | custom-call | flops 100000000 | bytes 10000 | tf_op jit(solution)/shard_map/pallas_call | solution.py:368
  19.0 8.7 %all-to-all-done.arrived = f32[64,8,128]{2,1,0:T(8,128)S(1)} async-done(((f32[64,8,128]{2,1,0:T(8,128)}), f32[64,8,128]{2,1,0:T(8,128)S(1)}, u32[]{:S(2)}, u32[]{:S(2)}) %all-to-all-start) | async-done | bytes 262176 | tf_op jit(solution)/shard_map/all_to_all | solution.py:437
  27.7 2.0 %shard_map.123 = (f32[65,8,128]{2,1,0:T(8,128)S(1)}, f32[64,2,640]{2,1,0:T(2,128)}) custom-call(s32[8,128]{1,0:T(8,128)S(1)} %shard_map.121.table, f32[64,8,128]{2,1,0:T(8,128)S(1)} %get-tuple-element.13.states, f32[64,8,128]{2,1,0:T(8,128)S(1)} %all-to-all-done.arrived), custom_call_target="tpu_custom_call" | custom-call | tf_op jit(solution)/shard_map/pallas_call | solution.py:381
  29.7 6.0 %all-to-all-start.1 = ((f32[64,2,640]{2,1,0:T(2,128)}), f32[64,2,640]{2,1,0:T(2,128)S(1)}, u32[]{:S(2)}, u32[]{:S(2)}) async-start(f32[64,2,640]{2,1,0:T(2,128)} %get-tuple-element.18), calls=%async_computation.1 | async-start | bytes 655360 | tf_op jit(solution)/shard_map/all_to_all | solution.py:437
  35.7 8.8 %shard_map.124 = (f32[64,16,128]{2,1,0:T(8,128)S(1)}, bf16[64,32,128]{2,1,0:T(8,128)(2,1)S(1)}) custom-call(s32[8,128]{1,0:T(8,128)S(1)} %shard_map.121.table, f32[65,8,128]{2,1,0:T(8,128)S(1)} %get-tuple-element.15.placed), custom_call_target="tpu_custom_call" | custom-call | flops 1000000000 | bytes 1000000 | tf_op jit(solution)/shard_map/pallas_call | solution.py:391
  44.5 3.7 %all-to-all-done.1.received.earlier = f32[64,2,640]{2,1,0:T(2,128)S(1)} async-done(((f32[64,2,640]{2,1,0:T(2,128)}), f32[64,2,640]{2,1,0:T(2,128)S(1)}, u32[]{:S(2)}, u32[]{:S(2)}) %all-to-all-start.1) | async-done | bytes 327712 | tf_op jit(solution)/shard_map/all_to_all | solution.py:437
  48.2 6.1 %shard_map.125 = (f32[65,8,128]{2,1,0:T(8,128)S(1)}, f32[64,2,384]{2,1,0:T(2,128)}) custom-call(s32[8,128]{1,0:T(8,128)S(1)} %shard_map.121.table, f32[65,8,128]{2,1,0:T(8,128)S(1)} %get-tuple-element.15.placed, f32[64,16,128]{2,1,0:T(8,128)S(1)} %get-tuple-element.16.sums, bf16[64,32,128]{2,1,0:T(8,128)(2,1)S(1)} %get-tuple-element.17.targets, ...), custom_call_target="tpu_custom_call" | custom-call | tf_op jit(solution)/shard_map/pallas_call | solution.py:410
  54.3 7.0 %all-to-all-start.2 = ((f32[64,2,384]{2,1,0:T(2,128)}), f32[64,2,384]{2,1,0:T(2,128)S(1)}, u32[]{:S(2)}, u32[]{:S(2)}) async-start(f32[64,2,384]{2,1,0:T(2,128)} %get-tuple-element.22), calls=%async_computation.2 | async-start | bytes 393216 | tf_op jit(solution)/shard_map/all_to_all | solution.py:437
  61.4 8.7 %shard_map.126 = (f32[64,16,128]{2,1,0:T(8,128)S(1)}, bf16[64,32,128]{2,1,0:T(8,128)(2,1)S(1)}) custom-call(s32[8,128]{1,0:T(8,128)S(1)} %shard_map.121.table, f32[65,8,128]{2,1,0:T(8,128)S(1)} %get-tuple-element.19.placed), custom_call_target="tpu_custom_call" | custom-call | flops 1000000000 | bytes 1000000 | tf_op jit(solution)/shard_map/pallas_call | solution.py:391
  70.1 1.6 %all-to-all-done.2.received = f32[64,2,384]{2,1,0:T(2,128)S(1)} async-done(((f32[64,2,384]{2,1,0:T(2,128)}), f32[64,2,384]{2,1,0:T(2,128)S(1)}, u32[]{:S(2)}, u32[]{:S(2)}) %all-to-all-start.2) | async-done | bytes 196640 | tf_op jit(solution)/shard_map/all_to_all | solution.py:437
  71.7 5.8 %shard_map.127 = (f32[3,8192]{1,0:T(4,128)}, f32[3,8192]{1,0:T(4,128)}, f32[3,8192]{1,0:T(4,128)}) custom-call(s32[8,128]{1,0:T(8,128)S(1)} %shard_map.121.table, f32[65,8,128]{2,1,0:T(8,128)S(1)} %get-tuple-element.19.placed, f32[64,16,128]{2,1,0:T(8,128)S(1)} %get-tuple-element.20.sums, bf16[64,32,128]{2,1,0:T(8,128)(2,1)S(1)} %get-tuple-element.21.targets, ...), custom_call_target="tpu_custom_call" | custom-call | tf_op jit(solution)/shard_map/pallas_call | solution.py:424
Async XLA Ops:
  1.3 0.7 copy-start
  3.9 12.3 %copy-start.1 = (s32[1,192]{1,0:T(1,128)S(1)}, s32[1,192]{1,0:T(1,128)}, u32[]{:S(2)}) copy-start(s32[1,192]{1,0:T(1,128)} %home.1) | copy-start | bytes 2308
  3.9 12.3 %copy-start.2 = (s32[1,192]{1,0:T(1,128)S(1)}, s32[1,192]{1,0:T(1,128)}, u32[]{:S(2)}) copy-start(s32[1,192]{1,0:T(1,128)} %other.1) | copy-start | bytes 2308
  3.9 12.3 %copy-start.3 = (s32[1,64]{1,0:T(1,128)S(1)}, s32[1,64]{1,0:T(1,128)}, u32[]{:S(2)}) copy-start(s32[1,64]{1,0:T(1,128)} %land.1) | copy-start | bytes 772
  3.9 12.3 %copy-start.4 = (s32[1,64]{1,0:T(1,128)S(1)}, s32[1,64]{1,0:T(1,128)}, u32[]{:S(2)}) copy-start(s32[1,64]{1,0:T(1,128)} %ghost.1) | copy-start | bytes 772
  3.9 23.8 %all-to-all-start = ((f32[64,8,128]{2,1,0:T(8,128)}), f32[64,8,128]{2,1,0:T(8,128)S(1)}, u32[]{:S(2)}, u32[]{:S(2)}) async-start(f32[64,8,128]{2,1,0:T(8,128)} %get-tuple-element.14), calls=%async_computation | async-start | bytes 524288 | tf_op jit(solution)/shard_map/all_to_all | solution.py:437
  29.7 18.5 %all-to-all-start.1 = ((f32[64,2,640]{2,1,0:T(2,128)}), f32[64,2,640]{2,1,0:T(2,128)S(1)}, u32[]{:S(2)}, u32[]{:S(2)}) async-start(f32[64,2,640]{2,1,0:T(2,128)} %get-tuple-element.18), calls=%async_computation.1 | async-start | bytes 655360 | tf_op jit(solution)/shard_map/all_to_all | solution.py:437
  54.3 17.4 %all-to-all-start.2 = ((f32[64,2,384]{2,1,0:T(2,128)}), f32[64,2,384]{2,1,0:T(2,128)S(1)}, u32[]{:S(2)}, u32[]{:S(2)}) async-start(f32[64,2,384]{2,1,0:T(2,128)} %get-tuple-element.22), calls=%async_computation.2 | async-start | bytes 393216 | tf_op jit(solution)/shard_map/all_to_all | solution.py:437

commit v3 on v2

--- a/solution.py
+++ b/solution.py
@@ -8,16 +8,16 @@
 from jax.sharding import PartitionSpec as P
 
 BLOCK = 128
+HALF = BLOCK // 2
 BLOCKS = 64
 DOMAINS = 64
 LOCAL = 128
-LAND, SENT, MATE, HOME, OTHER = range(5)
 
 coupling_scale = 0.2
 time_step = 0.05
 root_log2e = math.sqrt(math.log2(math.e))
-local_unroll = 32
-ghost_unroll = 32
+local_unroll = 128
+ghost_unroll = 64
 f32 = jnp.float32
 bf16 = jnp.bfloat16
 
@@ -69,19 +69,25 @@
     low = row_masks()[2]
     ones = jnp.ones((1, BLOCK), f32)
     w0, w1, w2 = split3(jnp.concatenate([coords, ones, coords, ones], 0) * weight)
-    return jnp.concatenate([jnp.where(low, w0, w1), jnp.where(low, w2, 0.0)], 0).astype(bf16)
+    rows = jnp.concatenate([jnp.where(low, w0, w1), jnp.where(low, w2, 0.0)], 0)
+    turned = pltpu.roll(rows, HALF, 1)
+    early = lax.broadcasted_iota(jnp.int32, (16, BLOCK), 1) < HALF
+    return jnp.concatenate(
+        [jnp.where(early, rows, turned), jnp.where(early, turned, rows)], 1
+    ).astype(bf16)
 
 
 def coupled_sums(sources, charges, weights, targets, target_charges):
+    depth = sources.shape[1] // 2
     empty = jnp.zeros((32, BLOCK), bf16)
-    right = jnp.concatenate(
-        [
-            jnp.concatenate([targets[0], empty], 1),
-            jnp.concatenate([empty, targets[1]], 1),
-        ],
-        0,
-    )
-    exponent = jnp.dot(sources, right, preferred_element_type=f32)
+    right = [
+        jnp.concatenate([targets[0], empty], 1),
+        jnp.concatenate([empty, targets[1]], 1),
+    ]
+    if depth > 32:
+        gap = jnp.zeros((depth - 32, 2 * BLOCK), bf16)
+        right = [right[0], gap, right[1], gap]
+    exponent = jnp.dot(sources, jnp.concatenate(right, 0), preferred_element_type=f32)
     tiles = []
     for which in range(2):
         decay = jnp.exp2(exponent[:, which * BLOCK : (which + 1) * BLOCK])
@@ -89,9 +95,8 @@
     coupling = jnp.concatenate(tiles, 1)
     high = coupling.astype(bf16)
     low = (coupling - high.astype(f32)).astype(bf16)
-    stacked = jnp.concatenate([high, low], 0)
+    stacked = jnp.concatenate([high[:HALF], low[:HALF], high[HALF:], low[HALF:]], 0)
     left = jnp.concatenate(weights, 0)
-    left = jnp.concatenate([left, left], 1)
     return jnp.dot(left, stacked, preferred_element_type=f32)
 
 
@@ -126,21 +131,28 @@
     lax.fori_loop(0, DOMAINS // 8, hand_over, 0)
 
 
-def table_kernel(land, ghost, home, other, table):
-    def by_peer(peer, carry):
-        table[LAND, peer] = land[0, peer]
-        table[SENT, peer] = ghost[0, peer]
-        table[MATE, other[0, LOCAL + peer] - BLOCKS] = home[0, LOCAL + peer]
-        return carry
-
-    lax.fori_loop(0, DOMAINS, by_peer, 0)
-
-    def by_pair(entry, carry):
-        table[HOME, entry] = home[0, entry]
-        table[OTHER, entry] = other[0, entry]
-        return carry
-
-    lax.fori_loop(0, LOCAL, by_pair, 0)
+def table_kernel(land, ghost, home, other, local_table, ghost_table):
+    def by_pair(group, carry):
+        for inner in range(8):
+            entry = group * 8 + inner
+            local_table[0, entry] = home[0, entry] + BLOCKS * other[0, entry]
+        return carry
+
+    lax.fori_loop(0, LOCAL // 8, by_pair, 0)
+
+    def by_peer(group, carry):
+        for inner in range(8):
+            entry = LOCAL + group * 8 + inner
+            peer = other[0, entry] - BLOCKS
+            ghost_table[0, peer] = home[0, entry] + BLOCKS * (ghost[0, peer] + BLOCKS * land[0, peer])
+        return carry
+
+    lax.fori_loop(0, DOMAINS // 8, by_peer, 0)
+
+
+def pair_of(table, entry):
+    packed = table[0, entry]
+    return packed & (BLOCKS - 1), (packed >> 6) & (BLOCKS - 1)
 
 
 def place_kernel(table, states, arrived, placed, outgoing):
@@ -153,7 +165,7 @@
     def receive(group, carry):
         for inner in range(8):
             peer = group * 8 + inner
-            placed[table[LAND, peer]] = arrived[peer]
+            placed[table[0, peer] >> 12] = arrived[peer]
         return carry
 
     lax.fori_loop(0, DOMAINS // 8, receive, 0)
@@ -161,7 +173,8 @@
     def send(group, carry):
         for inner in range(8):
             peer = group * 8 + inner
-            for which, slot in enumerate((table[SENT, peer], table[MATE, peer])):
+            mate, sent = pair_of(table, peer)
+            for which, slot in enumerate((sent, mate)):
                 for column, row in enumerate((0, 1, 2, 6, 7)):
                     outgoing[peer, which : which + 1, column * BLOCK : (column + 1) * BLOCK] = (
                         placed[slot, row : row + 1, :]
@@ -171,7 +184,7 @@
     lax.fori_loop(0, DOMAINS // 8, send, 0)
 
 
-def local_kernel(table, placed, sums, targets, first, second, weights, spread):
+def local_kernel(table, placed, sums, targets, columns_of, weights, spread):
     def prepare(group):
         stacked = []
         for inner in range(4):
@@ -183,13 +196,11 @@
             stacked.append(source_rows(parts, state[6:7]))
             sums[block] = jnp.zeros((16, BLOCK), f32)
         columns = jnp.concatenate(stacked, 0).T
-        empty = jnp.zeros((BLOCK, 32), bf16)
+        empty = jnp.zeros((BLOCK, BLOCK - 32), bf16)
         for inner in range(4):
             block = group * 4 + inner
             chosen = columns[:, inner * 32 : (inner + 1) * 32]
-            narrow = chosen.astype(bf16)
-            first[block] = jnp.concatenate([narrow, empty], 1)
-            second[block] = jnp.concatenate([empty, narrow], 1)
+            columns_of[block] = jnp.concatenate([chosen.astype(bf16), empty], 1)
             spread[block] = jnp.broadcast_to(chosen[:, 24:25], (BLOCK, BLOCK))
 
     def prepare_some(chunk, carry):
@@ -202,10 +213,9 @@
     def pairs(group, carry):
         for inner in range(local_unroll):
             entry = group * local_unroll + inner
-            one = table[HOME, entry]
-            two = table[OTHER, entry]
+            one, two = pair_of(table, entry)
             result = coupled_sums(
-                first[two] + second[one],
+                jnp.concatenate([columns_of[two], columns_of[one]], 1),
                 (spread[two], spread[one]),
                 (weights[two], weights[one]),
                 (targets[one], targets[two]),
@@ -240,8 +250,7 @@
             narrow = columns.astype(bf16)
             for inner in range(2):
                 peer = group * ghost_unroll + half * 2 + inner
-                one = table[MATE, peer]
-                two = table[SENT, peer]
+                one, two = pair_of(table, peer)
                 lane = inner * 64
                 result = coupled_sums(
                     narrow[:, lane : lane + 64],
@@ -294,7 +303,8 @@
     def send(group, carry):
         for inner in range(8):
             peer = group * 8 + inner
-            for which, slot in enumerate((table[SENT, peer], table[MATE, peer])):
+            mate, sent = pair_of(table, peer)
+            for which, slot in enumerate((sent, mate)):
                 for column in range(3):
                     outgoing[peer, which : which + 1, column * BLOCK : (column + 1) * BLOCK] = (
                         updated[slot, column : column + 1, :]
@@ -361,7 +371,7 @@
         in_specs=[smem, smem, vmem, vmem, vmem, vmem],
         out_specs=(vmem, vmem),
         out_shape=(shape(BLOCKS, 8, BLOCK), shape(DOMAINS, 8, BLOCK)),
-    )(scale, send, *(in_hbm(x) for x in (positions, velocities, charges, solute)))
+    )(scale, *(in_hbm(x) for x in (send, positions, velocities, charges, solute)))
 
 
 def tables(land, ghost, home, other):
@@ -369,8 +379,8 @@
         table_kernel,
         compiler_params=grant(1),
         in_specs=[smem, smem, smem, smem],
-        out_specs=smem,
-        out_shape=shape(8, LOCAL, dtype=jnp.int32),
+        out_specs=(smem, smem),
+        out_shape=(shape(1, LOCAL, dtype=jnp.int32), shape(1, DOMAINS, dtype=jnp.int32)),
         cost_estimate=pl.CostEstimate(
             flops=100_000_000, transcendentals=0, bytes_accessed=10_000
         ),
@@ -395,9 +405,8 @@
         out_specs=(vmem, vmem),
         out_shape=(shape(BLOCKS, 16, BLOCK), shape(BLOCKS, 32, BLOCK, dtype=bf16)),
         scratch_shapes=[
-            pltpu.VMEM((BLOCKS, BLOCK, 64), bf16),
-            pltpu.VMEM((BLOCKS, BLOCK, 64), bf16),
-            pltpu.VMEM((BLOCKS, 16, BLOCK), bf16),
+            pltpu.VMEM((BLOCKS, BLOCK, BLOCK), bf16),
+            pltpu.VMEM((BLOCKS, 16, 2 * BLOCK), bf16),
             pltpu.VMEM((BLOCKS, BLOCK, BLOCK), f32),
         ],
         cost_estimate=pl.CostEstimate(
@@ -458,14 +467,14 @@
         solute.reshape(BLOCKS, BLOCK),
     )
     arrived = exchange(outbound)
-    table = tables(land_slot, ghost_slot, pair_home, pair_other)
-    placed, outgoing = place(table, states, arrived)
+    local_table, ghost_table = tables(land_slot, ghost_slot, pair_home, pair_other)
+    placed, outgoing = place(ghost_table, states, arrived)
     ghosts = exchange(outgoing)
-    sums, targets = local_pairs(table, placed)
-    placed, outgoing = middle(table, placed, sums, targets, ghosts)
+    sums, targets = local_pairs(local_table, placed)
+    placed, outgoing = middle(ghost_table, placed, sums, targets, ghosts)
     moved_ghosts = exchange(outgoing)
-    sums, targets = local_pairs(table, placed)
-    return last(table, placed, sums, targets, moved_ghosts, ghosts)
+    sums, targets = local_pairs(local_table, placed)
+    return last(ghost_table, placed, sums, targets, moved_ghosts, ghosts)
 
 
 def solution(mesh):

time: 77.9 us -> 75.7 us (0.972)
  Pallas kernels: 36.2 us -> 32.2 us
  waiting for transfers between devices: 14 us -> 17.4 us
  starting transfers between devices: 25.3 us -> 24.4 us
    all_to_all x3, waiting for transfers between devices: 14 us -> 17.4 us  [exchange(): lax.all_to_all(values, 'dom', split_axis=0, concat_axis=0, tiled=True)]
    pallas_call x2, Pallas kernels: 17.5 us -> 15.2 us  [local_pairs(): pl.pallas_call(local_kernel, compiler_params=grant(16), in_specs=[smem, v...]
    pallas_call x1, Pallas kernels: 2.81 us -> 1.74 us  [tables(): pl.pallas_call(table_kernel, compiler_params=grant(1), in_specs=[smem, sm...]
    all_to_all x3, starting transfers between devices: 25.3 us -> 24.4 us  [exchange(): lax.all_to_all(values, 'dom', split_axis=0, concat_axis=0, tiled=True)]
  transfers between devices with their start and end apart: 3 -> 3, of which waited for: 3 -> 3; matrix products, arithmetic and copies ran while one was open for 0% -> 0% of each run, Pallas kernels for 26% -> 22%
where the time goes in v3:
time: 75.7 us; the launch traced here: 75.4 us
  Pallas kernels  32.2 us (43%)
  starting transfers between devices  24.4 us (32%)
  waiting for transfers between devices  17.4 us (23%)
  between operations  1.36 us (2%)
    all_to_all x3, starting transfers between devices, exchange(): lax.all_to_all(values, 'dom', split_axis=0, concat_axis=0, tiled=True)  24.4 us
    all_to_all x3, waiting for transfers between devices, exchange(): lax.all_to_all(values, 'dom', split_axis=0, concat_axis=0, tiled=True)  17.4 us
    pallas_call x2, Pallas kernels, local_pairs(): pl.pallas_call(local_kernel, compiler_params=grant(16), in_specs=[smem, v...  15.2 us
    pallas_call x1, Pallas kernels, middle(): pl.pallas_call(middle_kernel, compiler_params=grant(8), in_specs=[smem, v...  5.81 us
    pallas_call x1, Pallas kernels, last(): pl.pallas_call(last_kernel, compiler_params=grant(8), in_specs=[smem, vme...  5.64 us
    pallas_call x1, Pallas kernels, pack(): pl.pallas_call(pack_kernel, compiler_params=grant(4), in_specs=[smem, sme...  1.96 us
    pallas_call x1, Pallas kernels, place(): pl.pallas_call(place_kernel, compiler_params=grant(4), in_specs=[smem, vm...  1.82 us
    pallas_call x1, Pallas kernels, tables(): pl.pallas_call(table_kernel, compiler_params=grant(1), in_specs=[smem, sm...  1.74 us
  transfers between devices with their start and end apart: 3, of which 3 were waited for; matrix products, arithmetic and copies ran while one was open for 0% of the time, Pallas kernels for 22%

profile of v3, /device:TPU:2, one launch (start us, length us, event | category | flops | bytes accessed | tf_op | source)
XLA Modules:
  0.0 75.4 jit_solution(768754150816349733)
XLA Ops:
  1.3 2.0 %shard_map.122 = (f32[64,8,128]{2,1,0:T(8,128)S(1)}, f32[64,8,128]{2,1,0:T(8,128)}) custom-call(f32[1]{0:T(128)S(6)} %copy.13.scale, s32[1,64]{1,0:T(1,128)} %send.1, f32[3,8192]{1,0:T(4,128)} %positions.1, f32[3,8192]{1,0:T(4,128)} %velocities.1, f32[64,128]{1,0:T(8,128)} %bitcast.2, s32[64,128]{1,0:T(8,128)} %bitcast.3), custom_call_target="tpu_custom_call" | custom-call | tf_op jit(solution)/shard_map/pallas_call | solution.py:368
  3.2 0.0 copy-start
  3.2 0.0 copy-start.1
  3.2 0.0 copy-start.2
  3.3 0.0 copy-start.3
  3.3 12.2 %all-to-all-start = ((f32[64,8,128]{2,1,0:T(8,128)}), f32[64,8,128]{2,1,0:T(8,128)S(1)}, u32[]{:S(2)}, u32[]{:S(2)}) async-start(f32[64,8,128]{2,1,0:T(8,128)} %get-tuple-element.17), calls=%async_computation | async-start | bytes 524288 | tf_op jit(solution)/shard_map/all_to_all | solution.py:446
  15.5 0.0 copy-done
  15.5 0.0 copy-done.1
  15.5 0.0 copy-done.2
  15.5 0.0 copy-done.3
  15.5 1.7 %shard_map.121 = (s32[1,128]{1,0:T(1,128)S(1)}, s32[1,64]{1,0:T(1,128)S(1)}) custom-call(s32[1,64]{1,0:T(1,128)S(1)} %copy-done.2, s32[1,64]{1,0:T(1,128)S(1)} %copy-done.3, s32[1,192]{1,0:T(1,128)S(1)} %copy-done, s32[1,192]{1,0:T(1,128)S(1)} %copy-done.1), custom_call_target="tpu_custom_call" | custom-call | flops 100000000 | bytes 10000 | tf_op jit(solution)/shard_map/pallas_call | solution.py:378
  17.3 9.8 %all-to-all-done.arrived = f32[64,8,128]{2,1,0:T(8,128)S(1)} async-done(((f32[64,8,128]{2,1,0:T(8,128)}), f32[64,8,128]{2,1,0:T(8,128)S(1)}, u32[]{:S(2)}, u32[]{:S(2)}) %all-to-all-start) | async-done | bytes 262176 | tf_op jit(solution)/shard_map/all_to_all | solution.py:446
  27.1 1.8 %shard_map.123 = (f32[65,8,128]{2,1,0:T(8,128)S(1)}, f32[64,2,640]{2,1,0:T(2,128)}) custom-call(s32[1,64]{1,0:T(1,128)S(1)} %get-tuple-element.15.table, f32[64,8,128]{2,1,0:T(8,128)S(1)} %get-tuple-element.16.states, f32[64,8,128]{2,1,0:T(8,128)S(1)} %all-to-all-done.arrived), custom_call_target="tpu_custom_call" | custom-call | tf_op jit(solution)/shard_map/pallas_call | solution.py:391
  28.9 6.0 %all-to-all-start.1 = ((f32[64,2,640]{2,1,0:T(2,128)}), f32[64,2,640]{2,1,0:T(2,128)S(1)}, u32[]{:S(2)}, u32[]{:S(2)}) async-start(f32[64,2,640]{2,1,0:T(2,128)} %get-tuple-element.22), calls=%async_computation.1 | async-start | bytes 655360 | tf_op jit(solution)/shard_map/all_to_all | solution.py:446
  34.9 7.6 %shard_map.124 = (f32[64,16,128]{2,1,0:T(8,128)S(1)}, bf16[64,32,128]{2,1,0:T(8,128)(2,1)S(1)}) custom-call(s32[1,128]{1,0:T(1,128)S(1)} %get-tuple-element.19.table, f32[65,8,128]{2,1,0:T(8,128)S(1)} %get-tuple-element.18.placed), custom_call_target="tpu_custom_call" | custom-call | flops 1000000000 | bytes 1000000 | tf_op jit(solution)/shard_map/pallas_call | solution.py:401
  42.5 4.9 %all-to-all-done.1.received.earlier = f32[64,2,640]{2,1,0:T(2,128)S(1)} async-done(((f32[64,2,640]{2,1,0:T(2,128)}), f32[64,2,640]{2,1,0:T(2,128)S(1)}, u32[]{:S(2)}, u32[]{:S(2)}) %all-to-all-start.1) | async-done | bytes 327712 | tf_op jit(solution)/shard_map/all_to_all | solution.py:446
  47.4 5.8 %shard_map.125 = (f32[65,8,128]{2,1,0:T(8,128)S(1)}, f32[64,2,384]{2,1,0:T(2,128)}) custom-call(s32[1,64]{1,0:T(1,128)S(1)} %get-tuple-element.15.table, f32[65,8,128]{2,1,0:T(8,128)S(1)} %get-tuple-element.18.placed, f32[64,16,128]{2,1,0:T(8,128)S(1)} %get-tuple-element.20.sums, bf16[64,32,128]{2,1,0:T(8,128)(2,1)S(1)} %get-tuple-element.21.targets, ...), custom_call_target="tpu_custom_call" | custom-call | tf_op jit(solution)/shard_map/pallas_call | solution.py:419
  53.2 6.2 %all-to-all-start.2 = ((f32[64,2,384]{2,1,0:T(2,128)}), f32[64,2,384]{2,1,0:T(2,128)S(1)}, u32[]{:S(2)}, u32[]{:S(2)}) async-start(f32[64,2,384]{2,1,0:T(2,128)} %get-tuple-element.26), calls=%async_computation.2 | async-start | bytes 393216 | tf_op jit(solution)/shard_map/all_to_all | solution.py:446
  59.4 7.6 %shard_map.126 = (f32[64,16,128]{2,1,0:T(8,128)S(1)}, bf16[64,32,128]{2,1,0:T(8,128)(2,1)S(1)}) custom-call(s32[1,128]{1,0:T(1,128)S(1)} %get-tuple-element.19.table, f32[65,8,128]{2,1,0:T(8,128)S(1)} %get-tuple-element.23.placed), custom_call_target="tpu_custom_call" | custom-call | flops 1000000000 | bytes 1000000 | tf_op jit(solution)/shard_map/pallas_call | solution.py:401
  67.0 2.7 %all-to-all-done.2.received = f32[64,2,384]{2,1,0:T(2,128)S(1)} async-done(((f32[64,2,384]{2,1,0:T(2,128)}), f32[64,2,384]{2,1,0:T(2,128)S(1)}, u32[]{:S(2)}, u32[]{:S(2)}) %all-to-all-start.2) | async-done | bytes 196640 | tf_op jit(solution)/shard_map/all_to_all | solution.py:446
  69.7 5.6 %shard_map.127 = (f32[3,8192]{1,0:T(4,128)}, f32[3,8192]{1,0:T(4,128)}, f32[3,8192]{1,0:T(4,128)}) custom-call(s32[1,64]{1,0:T(1,128)S(1)} %get-tuple-element.15.table, f32[65,8,128]{2,1,0:T(8,128)S(1)} %get-tuple-element.23.placed, f32[64,16,128]{2,1,0:T(8,128)S(1)} %get-tuple-element.24.sums, bf16[64,32,128]{2,1,0:T(8,128)(2,1)S(1)} %get-tuple-element.25.targets, ...), custom_call_target="tpu_custom_call" | custom-call | tf_op jit(solution)/shard_map/pallas_call | solution.py:433
Async XLA Ops:
  3.2 12.3 %copy-start = (s32[1,192]{1,0:T(1,128)S(1)}, s32[1,192]{1,0:T(1,128)}, u32[]{:S(2)}) copy-start(s32[1,192]{1,0:T(1,128)} %home.1) | copy-start | bytes 2308
  3.2 12.3 %copy-start.1 = (s32[1,192]{1,0:T(1,128)S(1)}, s32[1,192]{1,0:T(1,128)}, u32[]{:S(2)}) copy-start(s32[1,192]{1,0:T(1,128)} %other.1) | copy-start | bytes 2308
  3.2 12.3 %copy-start.2 = (s32[1,64]{1,0:T(1,128)S(1)}, s32[1,64]{1,0:T(1,128)}, u32[]{:S(2)}) copy-start(s32[1,64]{1,0:T(1,128)} %land.1) | copy-start | bytes 772
  3.3 12.3 %copy-start.3 = (s32[1,64]{1,0:T(1,128)S(1)}, s32[1,64]{1,0:T(1,128)}, u32[]{:S(2)}) copy-start(s32[1,64]{1,0:T(1,128)} %ghost.1) | copy-start | bytes 772
  3.3 23.8 %all-to-all-start = ((f32[64,8,128]{2,1,0:T(8,128)}), f32[64,8,128]{2,1,0:T(8,128)S(1)}, u32[]{:S(2)}, u32[]{:S(2)}) async-start(f32[64,8,128]{2,1,0:T(8,128)} %get-tuple-element.17), calls=%async_computation | async-start | bytes 524288 | tf_op jit(solution)/shard_map/all_to_all | solution.py:446
  28.9 18.5 %all-to-all-start.1 = ((f32[64,2,640]{2,1,0:T(2,128)}), f32[64,2,640]{2,1,0:T(2,128)S(1)}, u32[]{:S(2)}, u32[]{:S(2)}) async-start(f32[64,2,640]{2,1,0:T(2,128)} %get-tuple-element.22), calls=%async_computation.1 | async-start | bytes 655360 | tf_op jit(solution)/shard_map/all_to_all | solution.py:446
  53.2 16.5 %all-to-all-start.2 = ((f32[64,2,384]{2,1,0:T(2,128)}), f32[64,2,384]{2,1,0:T(2,128)S(1)}, u32[]{:S(2)}, u32[]{:S(2)}) async-start(f32[64,2,384]{2,1,0:T(2,128)} %get-tuple-element.26), calls=%async_computation.2 | async-start | bytes 393216 | tf_op jit(solution)/shard_map/all_to_all | solution.py:446

commit v4 on v3

--- a/solution.py
+++ b/solution.py
@@ -8,7 +8,6 @@
 from jax.sharding import PartitionSpec as P
 
 BLOCK = 128
-HALF = BLOCK // 2
 BLOCKS = 64
 DOMAINS = 64
 LOCAL = 128
@@ -25,6 +24,11 @@
 smem = pl.BlockSpec(memory_space=pltpu.SMEM)
 
 
+def repeat(count, body):
+    for index in range(count):
+        body(index, 0)
+
+
 def rounded(values):
     return values.astype(bf16).astype(f32)
 
@@ -69,12 +73,7 @@
     low = row_masks()[2]
     ones = jnp.ones((1, BLOCK), f32)
     w0, w1, w2 = split3(jnp.concatenate([coords, ones, coords, ones], 0) * weight)
-    rows = jnp.concatenate([jnp.where(low, w0, w1), jnp.where(low, w2, 0.0)], 0)
-    turned = pltpu.roll(rows, HALF, 1)
-    early = lax.broadcasted_iota(jnp.int32, (16, BLOCK), 1) < HALF
-    return jnp.concatenate(
-        [jnp.where(early, rows, turned), jnp.where(early, turned, rows)], 1
-    ).astype(bf16)
+    return jnp.concatenate([jnp.where(low, w0, w1), jnp.where(low, w2, 0.0)], 0).astype(bf16)
 
 
 def coupled_sums(sources, charges, weights, targets, target_charges):
@@ -95,8 +94,9 @@
     coupling = jnp.concatenate(tiles, 1)
     high = coupling.astype(bf16)
     low = (coupling - high.astype(f32)).astype(bf16)
-    stacked = jnp.concatenate([high[:HALF], low[:HALF], high[HALF:], low[HALF:]], 0)
+    stacked = jnp.concatenate([high, low], 0)
     left = jnp.concatenate(weights, 0)
+    left = jnp.concatenate([left, left], 1)
     return jnp.dot(left, stacked, preferred_element_type=f32)
 
 
@@ -104,11 +104,11 @@
     root = jnp.sqrt(jnp.full((8, BLOCK), scale[0], f32))
 
     def gather(group, carry):
-        first = pl.multiple_of(group * 8, 8)
+        first = group * 8
         charge_rows = charges[pl.ds(first, 8), :]
         weight = jnp.where(solute[pl.ds(first, 8), :] == 1, root, 1.0)
         for inner in range(8):
-            lanes = pl.ds(pl.multiple_of((group * 8 + inner) * BLOCK, BLOCK), BLOCK)
+            lanes = pl.ds((group * 8 + inner) * BLOCK, BLOCK)
             states[group * 8 + inner] = jnp.concatenate(
                 [
                     positions[:, lanes],
@@ -120,7 +120,7 @@
             )
         return carry
 
-    lax.fori_loop(0, BLOCKS // 8, gather, 0)
+    repeat(BLOCKS // 8, gather)
 
     def hand_over(group, carry):
         for inner in range(8):
@@ -128,7 +128,7 @@
             outbound[peer] = states[jnp.minimum(send[0, peer], BLOCKS - 1)]
         return carry
 
-    lax.fori_loop(0, DOMAINS // 8, hand_over, 0)
+    repeat(DOMAINS // 8, hand_over)
 
 
 def table_kernel(land, ghost, home, other, local_table, ghost_table):
@@ -160,7 +160,7 @@
         placed[pl.ds(group * 8, 8)] = states[pl.ds(group * 8, 8)]
         return carry
 
-    lax.fori_loop(0, BLOCKS // 8, keep, 0)
+    repeat(BLOCKS // 8, keep)
 
     def receive(group, carry):
         for inner in range(8):
@@ -168,7 +168,7 @@
             placed[table[0, peer] >> 12] = arrived[peer]
         return carry
 
-    lax.fori_loop(0, DOMAINS // 8, receive, 0)
+    repeat(DOMAINS // 8, receive)
 
     def send(group, carry):
         for inner in range(8):
@@ -181,7 +181,7 @@
                     )
         return carry
 
-    lax.fori_loop(0, DOMAINS // 8, send, 0)
+    repeat(DOMAINS // 8, send)
 
 
 def local_kernel(table, placed, sums, targets, columns_of, weights, spread):
@@ -204,11 +204,11 @@
             spread[block] = jnp.broadcast_to(chosen[:, 24:25], (BLOCK, BLOCK))
 
     def prepare_some(chunk, carry):
-        for inner in range(4):
-            prepare(chunk * 4 + inner)
-        return carry
-
-    lax.fori_loop(0, BLOCKS // 16, prepare_some, 0)
+        for inner in range(8):
+            prepare(chunk * 8 + inner)
+        return carry
+
+    lax.fori_loop(0, BLOCKS // 32, prepare_some, 0)
 
     def pairs(group, carry):
         for inner in range(local_unroll):
@@ -225,7 +225,7 @@
             sums[two] += result[16:, BLOCK:]
         return carry
 
-    lax.fori_loop(0, LOCAL // local_unroll, pairs, 0)
+    repeat(LOCAL // local_unroll, pairs)
 
 
 def ghost_pairs(table, placed, targets, sums, total, coords_of, params_of):
@@ -233,7 +233,7 @@
         total[pl.ds(group * 8, 8)] = sums[pl.ds(group * 8, 8)]
         return carry
 
-    lax.fori_loop(0, BLOCKS // 8, start, 0)
+    repeat(BLOCKS // 8, start)
 
     def pairs(group, carry):
         for half in range(ghost_unroll // 2):
@@ -266,7 +266,7 @@
                 total[two] += result[16:, BLOCK:]
         return carry
 
-    lax.fori_loop(0, DOMAINS // ghost_unroll, pairs, 0)
+    repeat(DOMAINS // ghost_unroll, pairs)
 
 
 def moved(state, total):
@@ -298,7 +298,7 @@
             updated[block] = jnp.concatenate([coords, speed, state[6:8]], 0)
         return carry
 
-    lax.fori_loop(0, BLOCKS // 8, step, 0)
+    repeat(BLOCKS // 8, step)
 
     def send(group, carry):
         for inner in range(8):
@@ -311,7 +311,7 @@
                     )
         return carry
 
-    lax.fori_loop(0, DOMAINS // 8, send, 0)
+    repeat(DOMAINS // 8, send)
 
 
 def last_kernel(
@@ -343,13 +343,13 @@
         for inner in range(8):
             block = group * 8 + inner
             coords, speed, force = moved(placed[block], total[block])
-            lanes = pl.ds(pl.multiple_of(block * BLOCK, BLOCK), BLOCK)
+            lanes = pl.ds(block * BLOCK, BLOCK)
             coords_out[:, lanes] = coords
             speeds_out[:, lanes] = speed
             forces_out[:, lanes] = force
         return carry
 
-    lax.fori_loop(0, BLOCKS // 8, step, 0)
+    repeat(BLOCKS // 8, step)
 
 
 def grant(mebibytes):
@@ -406,7 +406,7 @@
         out_shape=(shape(BLOCKS, 16, BLOCK), shape(BLOCKS, 32, BLOCK, dtype=bf16)),
         scratch_shapes=[
             pltpu.VMEM((BLOCKS, BLOCK, BLOCK), bf16),
-            pltpu.VMEM((BLOCKS, 16, 2 * BLOCK), bf16),
+            pltpu.VMEM((BLOCKS, 16, BLOCK), bf16),
             pltpu.VMEM((BLOCKS, BLOCK, BLOCK), f32),
         ],
         cost_estimate=pl.CostEstimate(

time: 75.7 us -> 74.9 us (0.989)
  Pallas kernels: 32.2 us -> 31.3 us
where the time goes in v4:
time: 74.9 us; the launch traced here: 74.6 us
  Pallas kernels  31.3 us (42%)
  starting transfers between devices  24.3 us (32%)
  waiting for transfers between devices  17.7 us (24%)
  between operations  1.36 us (2%)
    all_to_all x3, starting transfers between devices, exchange(): lax.all_to_all(values, 'dom', split_axis=0, concat_axis=0, tiled=True)  24.3 us
    all_to_all x3, waiting for transfers between devices, exchange(): lax.all_to_all(values, 'dom', split_axis=0, concat_axis=0, tiled=True)  17.7 us
    pallas_call x2, Pallas kernels, local_pairs(): pl.pallas_call(local_kernel, compiler_params=grant(16), in_specs=[smem, v...  14.9 us
    pallas_call x1, Pallas kernels, middle(): pl.pallas_call(middle_kernel, compiler_params=grant(8), in_specs=[smem, v...  5.76 us
    pallas_call x1, Pallas kernels, last(): pl.pallas_call(last_kernel, compiler_params=grant(8), in_specs=[smem, vme...  5.4 us
    pallas_call x1, Pallas kernels, pack(): pl.pallas_call(pack_kernel, compiler_params=grant(4), in_specs=[smem, sme...  1.8 us
    pallas_call x1, Pallas kernels, tables(): pl.pallas_call(table_kernel, compiler_params=grant(1), in_specs=[smem, sm...  1.74 us
    pallas_call x1, Pallas kernels, place(): pl.pallas_call(place_kernel, compiler_params=grant(4), in_specs=[smem, vm...  1.66 us
  transfers between devices with their start and end apart: 3, of which 3 were waited for; matrix products, arithmetic and copies ran while one was open for 0% of the time, Pallas kernels for 22%

profile of v4, /device:TPU:2, one launch (start us, length us, event | category | flops | bytes accessed | tf_op | source)
XLA Modules:
  0.0 74.6 jit_solution(4163746987397348031)
XLA Ops:
  1.3 1.8 %shard_map.122 = (f32[64,8,128]{2,1,0:T(8,128)S(1)}, f32[64,8,128]{2,1,0:T(8,128)}) custom-call(f32[1]{0:T(128)S(6)} %copy.13.scale, s32[1,64]{1,0:T(1,128)} %send.1, f32[3,8192]{1,0:T(4,128)} %positions.1, f32[3,8192]{1,0:T(4,128)} %velocities.1, f32[64,128]{1,0:T(8,128)} %bitcast.2, s32[64,128]{1,0:T(8,128)} %bitcast.3), custom_call_target="tpu_custom_call" | custom-call | tf_op jit(solution)/shard_map/pallas_call | solution.py:368
  3.1 0.0 copy-start
  3.1 0.0 copy-start.1
  3.1 0.0 copy-start.2
  3.1 0.0 copy-start.3
  3.1 12.2 %all-to-all-start = ((f32[64,8,128]{2,1,0:T(8,128)}), f32[64,8,128]{2,1,0:T(8,128)S(1)}, u32[]{:S(2)}, u32[]{:S(2)}) async-start(f32[64,8,128]{2,1,0:T(8,128)} %get-tuple-element.17), calls=%async_computation | async-start | bytes 524288 | tf_op jit(solution)/shard_map/all_to_all | solution.py:446
  15.3 0.0 copy-done
  15.3 0.0 copy-done.1
  15.4 0.0 copy-done.2
  15.4 0.0 copy-done.3
  15.4 1.7 %shard_map.121 = (s32[1,128]{1,0:T(1,128)S(1)}, s32[1,64]{1,0:T(1,128)S(1)}) custom-call(s32[1,64]{1,0:T(1,128)S(1)} %copy-done.2, s32[1,64]{1,0:T(1,128)S(1)} %copy-done.3, s32[1,192]{1,0:T(1,128)S(1)} %copy-done, s32[1,192]{1,0:T(1,128)S(1)} %copy-done.1), custom_call_target="tpu_custom_call" | custom-call | flops 100000000 | bytes 10000 | tf_op jit(solution)/shard_map/pallas_call | solution.py:378
  17.1 9.8 %all-to-all-done.arrived = f32[64,8,128]{2,1,0:T(8,128)S(1)} async-done(((f32[64,8,128]{2,1,0:T(8,128)}), f32[64,8,128]{2,1,0:T(8,128)S(1)}, u32[]{:S(2)}, u32[]{:S(2)}) %all-to-all-start) | async-done | bytes 262176 | tf_op jit(solution)/shard_map/all_to_all | solution.py:446
  26.9 1.7 %shard_map.123 = (f32[65,8,128]{2,1,0:T(8,128)S(1)}, f32[64,2,640]{2,1,0:T(2,128)}) custom-call(s32[1,64]{1,0:T(1,128)S(1)} %get-tuple-element.15.table, f32[64,8,128]{2,1,0:T(8,128)S(1)} %get-tuple-element.16.states, f32[64,8,128]{2,1,0:T(8,128)S(1)} %all-to-all-done.arrived), custom_call_target="tpu_custom_call" | custom-call | tf_op jit(solution)/shard_map/pallas_call | solution.py:391
  28.6 6.0 %all-to-all-start.1 = ((f32[64,2,640]{2,1,0:T(2,128)}), f32[64,2,640]{2,1,0:T(2,128)S(1)}, u32[]{:S(2)}, u32[]{:S(2)}) async-start(f32[64,2,640]{2,1,0:T(2,128)} %get-tuple-element.22), calls=%async_computation.1 | async-start | bytes 655360 | tf_op jit(solution)/shard_map/all_to_all | solution.py:446
  34.6 7.5 %shard_map.124 = (f32[64,16,128]{2,1,0:T(8,128)S(1)}, bf16[64,32,128]{2,1,0:T(8,128)(2,1)S(1)}) custom-call(s32[1,128]{1,0:T(1,128)S(1)} %get-tuple-element.19.table, f32[65,8,128]{2,1,0:T(8,128)S(1)} %get-tuple-element.18.placed), custom_call_target="tpu_custom_call" | custom-call | flops 1000000000 | bytes 1000000 | tf_op jit(solution)/shard_map/pallas_call | solution.py:401
  42.1 5.0 %all-to-all-done.1.received.earlier = f32[64,2,640]{2,1,0:T(2,128)S(1)} async-done(((f32[64,2,640]{2,1,0:T(2,128)}), f32[64,2,640]{2,1,0:T(2,128)S(1)}, u32[]{:S(2)}, u32[]{:S(2)}) %all-to-all-start.1) | async-done | bytes 327712 | tf_op jit(solution)/shard_map/all_to_all | solution.py:446
  47.1 5.8 %shard_map.125 = (f32[65,8,128]{2,1,0:T(8,128)S(1)}, f32[64,2,384]{2,1,0:T(2,128)}) custom-call(s32[1,64]{1,0:T(1,128)S(1)} %get-tuple-element.15.table, f32[65,8,128]{2,1,0:T(8,128)S(1)} %get-tuple-element.18.placed, f32[64,16,128]{2,1,0:T(8,128)S(1)} %get-tuple-element.20.sums, bf16[64,32,128]{2,1,0:T(8,128)(2,1)S(1)} %get-tuple-element.21.targets, ...), custom_call_target="tpu_custom_call" | custom-call | tf_op jit(solution)/shard_map/pallas_call | solution.py:419
  52.8 6.0 %all-to-all-start.2 = ((f32[64,2,384]{2,1,0:T(2,128)}), f32[64,2,384]{2,1,0:T(2,128)S(1)}, u32[]{:S(2)}, u32[]{:S(2)}) async-start(f32[64,2,384]{2,1,0:T(2,128)} %get-tuple-element.26), calls=%async_computation.2 | async-start | bytes 393216 | tf_op jit(solution)/shard_map/all_to_all | solution.py:446
  58.9 7.5 %shard_map.126 = (f32[64,16,128]{2,1,0:T(8,128)S(1)}, bf16[64,32,128]{2,1,0:T(8,128)(2,1)S(1)}) custom-call(s32[1,128]{1,0:T(1,128)S(1)} %get-tuple-element.19.table, f32[65,8,128]{2,1,0:T(8,128)S(1)} %get-tuple-element.23.placed), custom_call_target="tpu_custom_call" | custom-call | flops 1000000000 | bytes 1000000 | tf_op jit(solution)/shard_map/pallas_call | solution.py:401
  66.3 2.8 %all-to-all-done.2.received = f32[64,2,384]{2,1,0:T(2,128)S(1)} async-done(((f32[64,2,384]{2,1,0:T(2,128)}), f32[64,2,384]{2,1,0:T(2,128)S(1)}, u32[]{:S(2)}, u32[]{:S(2)}) %all-to-all-start.2) | async-done | bytes 196640 | tf_op jit(solution)/shard_map/all_to_all | solution.py:446
  69.2 5.4 %shard_map.127 = (f32[3,8192]{1,0:T(4,128)}, f32[3,8192]{1,0:T(4,128)}, f32[3,8192]{1,0:T(4,128)}) custom-call(s32[1,64]{1,0:T(1,128)S(1)} %get-tuple-element.15.table, f32[65,8,128]{2,1,0:T(8,128)S(1)} %get-tuple-element.23.placed, f32[64,16,128]{2,1,0:T(8,128)S(1)} %get-tuple-element.24.sums, bf16[64,32,128]{2,1,0:T(8,128)(2,1)S(1)} %get-tuple-element.25.targets, ...), custom_call_target="tpu_custom_call" | custom-call | tf_op jit(solution)/shard_map/pallas_call | solution.py:433
Async XLA Ops:
  3.1 12.3 %copy-start = (s32[1,192]{1,0:T(1,128)S(1)}, s32[1,192]{1,0:T(1,128)}, u32[]{:S(2)}) copy-start(s32[1,192]{1,0:T(1,128)} %home.1) | copy-start | bytes 2308
  3.1 12.3 %copy-start.1 = (s32[1,192]{1,0:T(1,128)S(1)}, s32[1,192]{1,0:T(1,128)}, u32[]{:S(2)}) copy-start(s32[1,192]{1,0:T(1,128)} %other.1) | copy-start | bytes 2308
  3.1 12.3 %copy-start.2 = (s32[1,64]{1,0:T(1,128)S(1)}, s32[1,64]{1,0:T(1,128)}, u32[]{:S(2)}) copy-start(s32[1,64]{1,0:T(1,128)} %land.1) | copy-start | bytes 772
  3.1 12.3 %copy-start.3 = (s32[1,64]{1,0:T(1,128)S(1)}, s32[1,64]{1,0:T(1,128)}, u32[]{:S(2)}) copy-start(s32[1,64]{1,0:T(1,128)} %ghost.1) | copy-start | bytes 772
  3.1 23.8 %all-to-all-start = ((f32[64,8,128]{2,1,0:T(8,128)}), f32[64,8,128]{2,1,0:T(8,128)S(1)}, u32[]{:S(2)}, u32[]{:S(2)}) async-start(f32[64,8,128]{2,1,0:T(8,128)} %get-tuple-element.17), calls=%async_computation | async-start | bytes 524288 | tf_op jit(solution)/shard_map/all_to_all | solution.py:446
  28.6 18.5 %all-to-all-start.1 = ((f32[64,2,640]{2,1,0:T(2,128)}), f32[64,2,640]{2,1,0:T(2,128)S(1)}, u32[]{:S(2)}, u32[]{:S(2)}) async-start(f32[64,2,640]{2,1,0:T(2,128)} %get-tuple-element.22), calls=%async_computation.1 | async-start | bytes 655360 | tf_op jit(solution)/shard_map/all_to_all | solution.py:446
  52.8 16.3 %all-to-all-start.2 = ((f32[64,2,384]{2,1,0:T(2,128)}), f32[64,2,384]{2,1,0:T(2,128)S(1)}, u32[]{:S(2)}, u32[]{:S(2)}) async-start(f32[64,2,384]{2,1,0:T(2,128)} %get-tuple-element.26), calls=%async_computation.2 | async-start | bytes 393216 | tf_op jit(solution)/shard_map/all_to_all | solution.py:446

commit v5 on v4

--- a/solution.py
+++ b/solution.py
@@ -76,17 +76,69 @@
     return jnp.concatenate([jnp.where(low, w0, w1), jnp.where(low, w2, 0.0)], 0).astype(bf16)
 
 
-def coupled_sums(sources, charges, weights, targets, target_charges):
-    depth = sources.shape[1] // 2
+def paired_targets(parts):
+    p0, p1, p2 = parts
+    third, last, low = row_masks()
+    fourth = third | last
+    plain = jnp.where(fourth, 1.0, p0)
+    steps = [
+        plain,
+        jnp.where(fourth, 1.0, p1),
+        plain,
+        jnp.where(fourth, -p0, p1),
+        jnp.where(fourth, -p1, p2),
+        jnp.where(fourth, -p2, p0),
+    ]
+    rest = [jnp.zeros((16, BLOCK), f32)]
+    upper = jnp.concatenate([jnp.where(low, step, 0.0) for step in steps] + rest, 0)
+    lower = jnp.concatenate([jnp.where(low, 0.0, step) for step in steps] + rest, 0)
+    return upper.astype(bf16), lower.astype(bf16)
+
+
+def paired_sources(coords, charges):
+    third, last, low = row_masks()
+    fourth = third | last
+    rows = []
+    for values in coords:
+        scaled = values * root_log2e
+        rows += [scaled, 0.5 * jnp.sum(scaled * scaled, 0, keepdims=True)]
+    p0, p1, p2 = split3(jnp.concatenate(rows, 0))
+    return [
+        jnp.where(fourth, -p0, p0),
+        jnp.where(fourth, -p1, p0),
+        jnp.where(fourth, -p2, p1),
+        jnp.where(fourth, 1.0, p1),
+        jnp.where(fourth, 1.0, p0),
+        jnp.where(fourth, 1.0, p2),
+        jnp.where(low, charges[0], charges[1]),
+        jnp.zeros((8, BLOCK), f32),
+    ]
+
+
+def paired_weights(coords, weights):
+    low = row_masks()[2]
+    ones = jnp.ones((1, BLOCK), f32)
+    rows = jnp.concatenate([coords[0], ones, coords[1], ones], 0)
+    parts = split3(rows * jnp.where(low, weights[0], weights[1]))
+    return jnp.concatenate([*parts, jnp.zeros((8, BLOCK), f32)], 0).astype(bf16)
+
+
+def local_right(targets):
     empty = jnp.zeros((32, BLOCK), bf16)
-    right = [
-        jnp.concatenate([targets[0], empty], 1),
-        jnp.concatenate([empty, targets[1]], 1),
-    ]
-    if depth > 32:
-        gap = jnp.zeros((depth - 32, 2 * BLOCK), bf16)
-        right = [right[0], gap, right[1], gap]
-    exponent = jnp.dot(sources, jnp.concatenate(right, 0), preferred_element_type=f32)
+    gap = jnp.zeros((BLOCK - 32, 2 * BLOCK), bf16)
+    return jnp.concatenate(
+        [
+            jnp.concatenate([targets[0], empty], 1),
+            gap,
+            jnp.concatenate([empty, targets[1]], 1),
+            gap,
+        ],
+        0,
+    )
+
+
+def coupled_sums(sources, charges, left, right, target_charges):
+    exponent = jnp.dot(sources, right, preferred_element_type=f32)
     tiles = []
     for which in range(2):
         decay = jnp.exp2(exponent[:, which * BLOCK : (which + 1) * BLOCK])
@@ -95,7 +147,6 @@
     high = coupling.astype(bf16)
     low = (coupling - high.astype(f32)).astype(bf16)
     stacked = jnp.concatenate([high, low], 0)
-    left = jnp.concatenate(weights, 0)
     left = jnp.concatenate([left, left], 1)
     return jnp.dot(left, stacked, preferred_element_type=f32)
 
@@ -184,7 +235,7 @@
     repeat(DOMAINS // 8, send)
 
 
-def local_kernel(table, placed, sums, targets, columns_of, weights, spread):
+def local_kernel(table, placed, sums, paired, targets, columns_of, weights, spread):
     def prepare(group):
         stacked = []
         for inner in range(4):
@@ -192,6 +243,7 @@
             state = placed[block]
             parts = exponent_parts(state[0:3])
             targets[block] = target_rows(parts)
+            paired[block, 0], paired[block, 1] = paired_targets(parts)
             weights[block] = weight_rows(state[0:3], state[7:8])
             stacked.append(source_rows(parts, state[6:7]))
             sums[block] = jnp.zeros((16, BLOCK), f32)
@@ -217,8 +269,8 @@
             result = coupled_sums(
                 jnp.concatenate([columns_of[two], columns_of[one]], 1),
                 (spread[two], spread[one]),
-                (weights[two], weights[one]),
-                (targets[one], targets[two]),
+                jnp.concatenate([weights[two], weights[one]], 0),
+                local_right((targets[one], targets[two])),
                 (placed[one, 6:7, :], placed[two, 6:7, :]),
             )
             sums[one] += result[:16, :BLOCK]
@@ -238,14 +290,13 @@
     def pairs(group, carry):
         for half in range(ghost_unroll // 2):
             stacked = []
-            weights = []
+            lefts = []
             for inner in range(2):
                 peer = group * ghost_unroll + half * 2 + inner
-                for which in range(2):
-                    coords = coords_of(peer, which)
-                    charge, weight = params_of(peer, which)
-                    stacked.append(source_rows(exponent_parts(coords), charge))
-                    weights.append(weight_rows(coords, weight))
+                coords = [coords_of(peer, which) for which in range(2)]
+                params = [params_of(peer, which) for which in range(2)]
+                stacked += paired_sources(coords, [param[0] for param in params])
+                lefts.append(paired_weights(coords, [param[1] for param in params]))
             columns = jnp.concatenate(stacked, 0).T
             narrow = columns.astype(bf16)
             for inner in range(2):
@@ -255,15 +306,17 @@
                 result = coupled_sums(
                     narrow[:, lane : lane + 64],
                     (
-                        jnp.broadcast_to(columns[:, lane + 24 : lane + 25], (BLOCK, BLOCK)),
-                        jnp.broadcast_to(columns[:, lane + 56 : lane + 57], (BLOCK, BLOCK)),
+                        jnp.broadcast_to(columns[:, lane + 48 : lane + 49], (BLOCK, BLOCK)),
+                        jnp.broadcast_to(columns[:, lane + 52 : lane + 53], (BLOCK, BLOCK)),
                     ),
-                    (weights[inner * 2], weights[inner * 2 + 1]),
-                    (targets[one], targets[two]),
+                    lefts[inner],
+                    jnp.concatenate([targets[one, 0], targets[two, 1]], 1),
                     (placed[one, 6:7, :], placed[two, 6:7, :]),
                 )
-                total[one] += result[:16, :BLOCK]
-                total[two] += result[16:, BLOCK:]
+                folded = result[0:8] + result[8:16] + result[16:24]
+                upper = row_masks()[2]
+                total[one, 0:8] += jnp.where(upper, folded[:, :BLOCK], 0.0)
+                total[two, 0:8] += jnp.where(upper, 0.0, folded[:, BLOCK:])
         return carry
 
     repeat(DOMAINS // ghost_unroll, pairs)
@@ -403,8 +456,9 @@
         compiler_params=grant(16),
         in_specs=[smem, vmem],
         out_specs=(vmem, vmem),
-        out_shape=(shape(BLOCKS, 16, BLOCK), shape(BLOCKS, 32, BLOCK, dtype=bf16)),
+        out_shape=(shape(BLOCKS, 16, BLOCK), shape(BLOCKS, 2, 64, BLOCK, dtype=bf16)),
         scratch_shapes=[
+            pltpu.VMEM((BLOCKS, 32, BLOCK), bf16),
             pltpu.VMEM((BLOCKS, BLOCK, BLOCK), bf16),
             pltpu.VMEM((BLOCKS, 16, BLOCK), bf16),
             pltpu.VMEM((BLOCKS, BLOCK, BLOCK), f32),
@@ -425,7 +479,7 @@
         scratch_shapes=[
             pltpu.VMEM((BLOCKS, 16, BLOCK), f32),
         ],
-    )(table, placed, sums, targets, received)
+    )(table, pltpu.with_memory_space_constraint(placed, pltpu.VMEM), sums, targets, received)
 
 
 def last(table, placed, sums, targets, received, earlier):

time: 74.9 us -> 75.1 us (level)
  local copies, waits for them, and re-layouts: 0.02 us -> 3.62 us
  waiting for transfers between devices: 17.7 us -> 14.7 us
    unnamed x8 -> x12, local copies, waits for them, and re-layouts: 0.02 us -> 3.62 us
    all_to_all x3, waiting for transfers between devices: 17.7 us -> 14.7 us  [exchange(): lax.all_to_all(values, 'dom', split_axis=0, concat_axis=0, tiled=True)]
  transfers between devices with their start and end apart: 3 -> 3, of which waited for: 3 -> 3; matrix products, arithmetic and copies ran while one was open for 0% -> 0% of each run, Pallas kernels for 22% -> 23%
where the time goes in v5:
time: 75.1 us; the launch traced here: 74.7 us
  Pallas kernels  31 us (41%)
  starting transfers between devices  24.1 us (32%)
  waiting for transfers between devices  14.7 us (20%)
  local copies, waits for them, and re-layouts  3.62 us (5%)
  between operations  1.34 us (2%)
    all_to_all x3, starting transfers between devices, exchange(): lax.all_to_all(values, 'dom', split_axis=0, concat_axis=0, tiled=True)  24.1 us
    pallas_call x2, Pallas kernels, local_pairs(): pl.pallas_call(local_kernel, compiler_params=grant(16), in_specs=[smem, v...  15.3 us
    all_to_all x3, waiting for transfers between devices, exchange(): lax.all_to_all(values, 'dom', split_axis=0, concat_axis=0, tiled=True)  14.7 us
    pallas_call x1, Pallas kernels, middle(): pl.pallas_call(middle_kernel, compiler_params=grant(8), in_specs=[smem, v...  5.34 us
    pallas_call x1, Pallas kernels, last(): pl.pallas_call(last_kernel, compiler_params=grant(8), in_specs=[smem, vme...  5.19 us
    unnamed x12, local copies, waits for them, and re-layouts  3.62 us
    pallas_call x1, Pallas kernels, pack(): pl.pallas_call(pack_kernel, compiler_params=grant(4), in_specs=[smem, sme...  1.79 us
    pallas_call x1, Pallas kernels, tables(): pl.pallas_call(table_kernel, compiler_params=grant(1), in_specs=[smem, sm...  1.74 us
  transfers between devices with their start and end apart: 3, of which 3 were waited for; matrix products, arithmetic and copies ran while one was open for 0% of the time, Pallas kernels for 23%

profile of v5, /device:TPU:2, one launch (start us, length us, event | category | flops | bytes accessed | tf_op | source)
XLA Modules:
  0.0 74.7 jit_solution(9188283893837958240)
XLA Ops:
  1.3 1.8 %shard_map.122 = (f32[64,8,128]{2,1,0:T(8,128)S(1)}, f32[64,8,128]{2,1,0:T(8,128)}) custom-call(f32[1]{0:T(128)S(6)} %copy.13.scale, s32[1,64]{1,0:T(1,128)} %send.1, f32[3,8192]{1,0:T(4,128)} %positions.1, f32[3,8192]{1,0:T(4,128)} %velocities.1, f32[64,128]{1,0:T(8,128)} %bitcast.2, s32[64,128]{1,0:T(8,128)} %bitcast.3), custom_call_target="tpu_custom_call" | custom-call | tf_op jit(solution)/shard_map/pallas_call | solution.py:421
  3.1 12.1 %all-to-all-start = ((f32[64,8,128]{2,1,0:T(8,128)}), f32[64,8,128]{2,1,0:T(8,128)S(1)}, u32[]{:S(2)}, u32[]{:S(2)}) async-start(f32[64,8,128]{2,1,0:T(8,128)} %get-tuple-element.17), calls=%async_computation | async-start | bytes 524288 | tf_op jit(solution)/shard_map/all_to_all | solution.py:500
  15.2 0.0 copy-start.2
  15.2 0.7 copy-done.2
  15.8 0.0 copy-start.3
  15.8 0.7 copy-done.3
  16.5 0.0 copy-start.4
  16.5 0.7 copy-done.4
  17.2 0.0 copy-start.5
  17.2 0.7 copy-done.5
  17.8 1.7 %shard_map.121 = (s32[1,128]{1,0:T(1,128)S(1)}, s32[1,64]{1,0:T(1,128)S(1)}) custom-call(s32[1,64]{1,0:T(1,128)S(1)} %copy-done.4, s32[1,64]{1,0:T(1,128)S(1)} %copy-done.5, s32[1,192]{1,0:T(1,128)S(1)} %copy-done.2, s32[1,192]{1,0:T(1,128)S(1)} %copy-done.3), custom_call_target="tpu_custom_call" | custom-call | flops 100000000 | bytes 10000 | tf_op jit(solution)/shard_map/pallas_call | solution.py:431
  19.6 7.2 %all-to-all-done.arrived = f32[64,8,128]{2,1,0:T(8,128)S(1)} async-done(((f32[64,8,128]{2,1,0:T(8,128)}), f32[64,8,128]{2,1,0:T(8,128)S(1)}, u32[]{:S(2)}, u32[]{:S(2)}) %all-to-all-start) | async-done | bytes 262176 | tf_op jit(solution)/shard_map/all_to_all | solution.py:500
  26.7 1.7 %shard_map.123 = (f32[65,8,128]{2,1,0:T(8,128)S(1)}, f32[64,2,640]{2,1,0:T(2,128)}) custom-call(s32[1,64]{1,0:T(1,128)S(1)} %get-tuple-element.15.table, f32[64,8,128]{2,1,0:T(8,128)S(1)} %get-tuple-element.16.states, f32[64,8,128]{2,1,0:T(8,128)S(1)} %all-to-all-done.arrived), custom_call_target="tpu_custom_call" | custom-call | tf_op jit(solution)/shard_map/pallas_call | solution.py:444
  28.4 0.0 copy-start
  28.4 6.0 %all-to-all-start.1 = ((f32[64,2,640]{2,1,0:T(2,128)}), f32[64,2,640]{2,1,0:T(2,128)S(1)}, u32[]{:S(2)}, u32[]{:S(2)}) async-start(f32[64,2,640]{2,1,0:T(2,128)} %get-tuple-element.22), calls=%async_computation.1 | async-start | bytes 655360 | tf_op jit(solution)/shard_map/all_to_all | solution.py:500
  34.4 7.6 %shard_map.124 = (f32[64,16,128]{2,1,0:T(8,128)S(1)}, bf16[64,2,64,128]{3,2,1,0:T(8,128)(2,1)S(1)}) custom-call(s32[1,128]{1,0:T(1,128)S(1)} %get-tuple-element.19.table, f32[65,8,128]{2,1,0:T(8,128)S(1)} %get-tuple-element.18.placed), custom_call_target="tpu_custom_call" | custom-call | flops 1000000000 | bytes 1000000 | tf_op jit(solution)/shard_map/pallas_call | solution.py:454
  42.1 0.0 copy-done
  42.1 4.8 %all-to-all-done.1.received.earlier = f32[64,2,640]{2,1,0:T(2,128)S(1)} async-done(((f32[64,2,640]{2,1,0:T(2,128)}), f32[64,2,640]{2,1,0:T(2,128)S(1)}, u32[]{:S(2)}, u32[]{:S(2)}) %all-to-all-start.1) | async-done | bytes 327712 | tf_op jit(solution)/shard_map/all_to_all | solution.py:500
  46.9 0.0 copy-start.1
  46.9 0.9 %copy-done.1 = f32[65,8,128]{2,1,0:T(8,128)S(1)} copy-done((f32[65,8,128]{2,1,0:T(8,128)S(1)}, f32[65,8,128]{2,1,0:T(8,128)}, u32[]{:S(2)}) %copy-start.1) | copy-done | bytes 266264
  47.9 5.3 %shard_map.125 = (f32[65,8,128]{2,1,0:T(8,128)S(1)}, f32[64,2,384]{2,1,0:T(2,128)}) custom-call(s32[1,64]{1,0:T(1,128)S(1)} %get-tuple-element.15.table, f32[65,8,128]{2,1,0:T(8,128)S(1)} %copy-done.1, f32[64,16,128]{2,1,0:T(8,128)S(1)} %get-tuple-element.20.sums, bf16[64,2,64,128]{3,2,1,0:T(8,128)(2,1)S(1)} %get-tuple-element.21.targets, ...), custom_call_target="tpu_custom_call" | custom-call | tf_op jit(solution)/shard_map/pallas_call | solution.py:473
  53.2 6.0 %all-to-all-start.2 = ((f32[64,2,384]{2,1,0:T(2,128)}), f32[64,2,384]{2,1,0:T(2,128)S(1)}, u32[]{:S(2)}, u32[]{:S(2)}) async-start(f32[64,2,384]{2,1,0:T(2,128)} %get-tuple-element.26), calls=%async_computation.2 | async-start | bytes 393216 | tf_op jit(solution)/shard_map/all_to_all | solution.py:500
  59.2 7.6 %shard_map.126 = (f32[64,16,128]{2,1,0:T(8,128)S(1)}, bf16[64,2,64,128]{3,2,1,0:T(8,128)(2,1)S(1)}) custom-call(s32[1,128]{1,0:T(1,128)S(1)} %get-tuple-element.19.table, f32[65,8,128]{2,1,0:T(8,128)S(1)} %get-tuple-element.23.placed), custom_call_target="tpu_custom_call" | custom-call | flops 1000000000 | bytes 1000000 | tf_op jit(solution)/shard_map/pallas_call | solution.py:454
  66.9 2.7 %all-to-all-done.2.received = f32[64,2,384]{2,1,0:T(2,128)S(1)} async-done(((f32[64,2,384]{2,1,0:T(2,128)}), f32[64,2,384]{2,1,0:T(2,128)S(1)}, u32[]{:S(2)}, u32[]{:S(2)}) %all-to-all-start.2) | async-done | bytes 196640 | tf_op jit(solution)/shard_map/all_to_all | solution.py:500
  69.6 5.2 %shard_map.127 = (f32[3,8192]{1,0:T(4,128)}, f32[3,8192]{1,0:T(4,128)}, f32[3,8192]{1,0:T(4,128)}) custom-call(s32[1,64]{1,0:T(1,128)S(1)} %get-tuple-element.15.table, f32[65,8,128]{2,1,0:T(8,128)S(1)} %get-tuple-element.23.placed, f32[64,16,128]{2,1,0:T(8,128)S(1)} %get-tuple-element.24.sums, bf16[64,2,64,128]{3,2,1,0:T(8,128)(2,1)S(1)} %get-tuple-element.25.targets, ...), custom_call_target="tpu_custom_call" | custom-call | tf_op jit(solution)/shard_map/pallas_call | solution.py:487
Async XLA Ops:
  3.1 23.7 %all-to-all-start = ((f32[64,8,128]{2,1,0:T(8,128)}), f32[64,8,128]{2,1,0:T(8,128)S(1)}, u32[]{:S(2)}, u32[]{:S(2)}) async-start(f32[64,8,128]{2,1,0:T(8,128)} %get-tuple-element.17), calls=%async_computation | async-start | bytes 524288 | tf_op jit(solution)/shard_map/all_to_all | solution.py:500
  15.2 0.7 copy-start.2
  15.8 0.7 copy-start.3
  16.5 0.7 copy-start.4
  17.2 0.7 copy-start.5
  28.4 13.7 %copy-start = (f32[65,8,128]{2,1,0:T(8,128)}, f32[65,8,128]{2,1,0:T(8,128)S(1)}, u32[]{:S(2)}) copy-start(f32[65,8,128]{2,1,0:T(8,128)S(1)} %get-tuple-element.18.placed) | copy-start | bytes 798724
  28.4 18.5 %all-to-all-start.1 = ((f32[64,2,640]{2,1,0:T(2,128)}), f32[64,2,640]{2,1,0:T(2,128)S(1)}, u32[]{:S(2)}, u32[]{:S(2)}) async-start(f32[64,2,640]{2,1,0:T(2,128)} %get-tuple-element.22), calls=%async_computation.1 | async-start | bytes 655360 | tf_op jit(solution)/shard_map/all_to_all | solution.py:500
  46.9 1.0 %copy-start.1 = (f32[65,8,128]{2,1,0:T(8,128)S(1)}, f32[65,8,128]{2,1,0:T(8,128)}, u32[]{:S(2)}) copy-start(f32[65,8,128]{2,1,0:T(8,128)} %copy-done) | copy-start | bytes 798724
  53.2 16.3 %all-to-all-start.2 = ((f32[64,2,384]{2,1,0:T(2,128)}), f32[64,2,384]{2,1,0:T(2,128)S(1)}, u32[]{:S(2)}, u32[]{:S(2)}) async-start(f32[64,2,384]{2,1,0:T(2,128)} %get-tuple-element.26), calls=%async_computation.2 | async-start | bytes 393216 | tf_op jit(solution)/shard_map/all_to_all | solution.py:500
